TPU v7x, 32 devices: a whole 2x2x4 slice. The times are simulated.
32 devices in a mesh: seq: 4 (over z), head: 4 (over y, core), batch: 2 (over x).
Axes of the slice: x: 2, y: 2, z: 4, core: 2. Of those that a mesh axis runs over, the one named last changes fastest.
Arguments:
- tokens: bfloat16 [8192, 2048], P(('batch', 'seq')), parts along dimension 0, may hold values from -6 to 6
- neighbor_bank: bfloat16 [128, 256, 2048], P(('batch', 'seq')), parts along dimension 0, may hold values from -2100 to 2100
- slots: int32 [128], P(('batch', 'seq')), parts along dimension 0, may hold values from 0 to 15
- w_query: bfloat16 [2048, 2048], P('seq', 'head'), may hold values from -0.125 to 0.125
- w_key: bfloat16 [2048, 2048], P('seq', 'head'), may hold values from -0.125 to 0.125
- w_value: bfloat16 [2048, 2048], P('seq', 'head'), may hold values from -0.125 to 0.125
- w_out: bfloat16 [2048, 2048], P('head', 'seq'), may hold values from -0.125 to 0.125
Outputs:
- cross_out: bfloat16 [8192, 2048], P(('batch', 'seq'), 'head'), parts along dimension 0
There are 2 independent parts, one for each index of `batch`. A program takes and returns all parts, laid end to end along the dimension named above; an argument that names none is the same for every part. Nothing has to cross between parts.
Inputs may be any that keep to these rules, and one draw needn't show every extreme that they name: Entry c picks row c // 16 * 16 + slots[c] of neighbor_bank.
All inputs are finite; a program needn't handle non-finite values.
Results may differ from a plain program's by a relative error of at most 0.006.
The roundings to bfloat16 on the way count: a program that leaves them out, or rounds other values in their place, can miss the bound.
Values may be sent and summed in bfloat16 or wider, within the bound.
A program may use at most 128 MiB of HBM per device.

v0:
```python
import functools
import math

import jax
import jax.numpy as jnp
from jax import lax
from jax.experimental import pallas as pl
from jax.experimental.pallas import tpu as pltpu
from jax.sharding import PartitionSpec as P

HEAD_DIM = 128
F32 = jnp.float32
BF16 = jnp.bfloat16


def fused(S, H, NS, tokens, bank, slots, w_query, w_key, w_value, w_out, out,
          G, WO, tok, normed, rows_in, kv, qb, halo_out, halo_in, att_own, att, acc,
          ld_sem, wl_sem, zr, xr, send_r, send_l, send_x, halo_s, halo_r,
          att_s, att_r, att_l, wo_s, wo_r, wo_l):
    s, h, b = lax.axis_index("seq"), lax.axis_index("head"), lax.axis_index("batch")
    nblk, nrow, D = bank.shape
    T = tokens.shape[0]
    blk = T // nblk
    CW = HEAD_DIM
    RS = w_query.shape[0]
    RH = RS // 2
    WH = CW // 2

    def dev(seq, head, batch):
        return {"seq": seq, "head": head, "batch": batch}

    def rcopy(src, dst, ss, rs, device):
        return pltpu.make_async_remote_copy(
            src_ref=src, dst_ref=dst, send_sem=ss, recv_sem=rs,
            device_id=device, device_id_type=pl.DeviceIdType.MESH)

    w_loads = []
    for k, w in enumerate((w_query, w_key, w_value)):
        for j in range(NS):
            c = pltpu.make_async_copy(
                w.at[:, pl.ds(j * CW, CW)],
                G.at[j, pl.ds(s * RS, RS), pl.ds(k * CW, CW)], wl_sem.at[k * NS + j])
            c.start()
            w_loads.append(c)
    tok_load = pltpu.make_async_copy(tokens, tok, ld_sem.at[nblk])
    tok_load.start()
    bank_loads = [pltpu.make_async_copy(bank.at[i], rows_in.at[i], ld_sem.at[i]) for i in range(nblk)]
    for c in bank_loads:
        c.start()

    barrier = pltpu.get_barrier_semaphore()
    for i in range(S):
        for k in range(H):
            @pl.when(jnp.logical_or(s != i, h != k))
            def _():
                pl.semaphore_signal(barrier, inc=1, device_id=dev(i, k, b), device_id_type=pl.DeviceIdType.MESH)
    pl.semaphore_signal(barrier, inc=1, device_id=dev(s, h, 1 - b), device_id_type=pl.DeviceIdType.MESH)
    pl.semaphore_wait(barrier, S * H)

    def chunk(t, origin, half):
        if isinstance(t, int) and t == NS:
            return wo_part(origin, half)
        return G.at[t, pl.ds(origin * RS + half * RH, RH), :]

    def right(t, origin):
        return rcopy(chunk(t, origin, b), chunk(t, origin, b), send_r.at[t, origin], zr.at[t, origin],
                     dev(lax.rem(s + 1, S), h, b))

    def left(t, origin):
        return rcopy(chunk(t, origin, b), chunk(t, origin, b), send_l.at[t, origin], zr.at[t, origin],
                     dev(lax.rem(s + S - 1, S), h, b))

    def twin(t, origin, half):
        return rcopy(chunk(t, origin, half), chunk(t, origin, half), send_x.at[t, origin], xr.at[t, origin],
                     dev(s, h, 1 - b))

    def send_own(t):
        @pl.when(s < S - 1)
        def _():
            right(t, s).start()

        @pl.when(s > 0)
        def _():
            left(t, s).start()

    def relay(t, d):
        @pl.when(s >= d)
        def _():
            right(t, s - d).wait_recv()

            @pl.when(s < S - 1)
            def _():
                right(t, s - d).start()
            twin(t, s - d, b).start()

        @pl.when(s + d < S)
        def _():
            left(t, s + d).wait_recv()

            @pl.when(s > 0)
            def _():
                left(t, s + d).start()
            twin(t, s + d, b).start()

    def wo_part(origin, half):
        return WO.at[:, pl.ds(origin * CW + half * WH, WH), :]

    def wo_turn(origin, device):
        return rcopy(w_out.at[:, pl.ds(b * WH, WH), :], wo_part(origin, b), wo_s, wo_r, device)

    wo_own = pltpu.make_async_copy(w_out, WO.at[:, pl.ds(h * CW, CW), :], wo_l)

    def attend(t, first_key, blocks):
        scores, probs = [], []
        for c, keys in blocks:
            q = qb[pl.ds(c * blk, blk), :]
            k = keys(0)
            scores.append(lax.dot_general(q, k, (((1,), (1,)), ((), ())), preferred_element_type=F32)
                          * (1.0 / math.sqrt(HEAD_DIM)))
        for sc in scores:
            e = jnp.exp(sc - jnp.max(sc, axis=-1, keepdims=True))
            probs.append((e / jnp.sum(e, axis=-1, keepdims=True)).astype(BF16))
        for (c, keys), p in zip(blocks, probs):
            o = jnp.dot(p, keys(1), preferred_element_type=F32)
            att_own[t, pl.ds(c * blk, blk), :] = o.astype(BF16)

    def halo(t):
        return rcopy(halo_out.at[t], halo_in.at[t], halo_s.at[t], halo_r.at[t], dev(lax.rem(s + 1, S), h, b))

    peers = ((h // 2) * 2 + 1 - lax.rem(h, 2), lax.rem(h + 2, H), lax.rem((h // 2) * 2 + 1 - lax.rem(h, 2) + 2, H))

    def att_send(t, k):
        return rcopy(att_own.at[t], att.at[t, :, pl.ds(h * CW, CW)], att_s.at[t, k], att_r.at[t, k],
                     dev(s, peers[k], b))

    def att_here(t):
        return pltpu.make_async_copy(att_own.at[t], att.at[t, :, pl.ds(h * CW, CW)], att_l.at[t])

    per = 4 if nblk % 4 == 0 else 1
    steps = nblk // per

    def project(t, lo, hi):
        def one(i, _):
            rows = rows_in[pl.ds(i * per, per)].reshape(per * nrow, D)
            kv[pl.ds(i * per, per)] = jnp.dot(
                rows, G[t, :, pl.ds(CW, 2 * CW)], preferred_element_type=F32).astype(BF16).reshape(per, nrow, 2 * CW)
            return 0
        lax.fori_loop(lo, hi, one, 0)

    def queries(t):
        qb[...] = jnp.dot(normed[...], G[t, :, pl.ds(0, CW)], preferred_element_type=F32).astype(BF16)

    for c in w_loads:
        c.wait()
    @pl.when(h != s)
    def _():
        wo_turn(h, dev(h, s, b)).start()

    @pl.when(h == s)
    def _():
        wo_own.start()
        wo_own.wait()
    send_own(0)
    send_own(1)

    @pl.when(s == 0)
    def _():
        halo_in[...] = jnp.zeros_like(halo_in)

    tok_load.wait()

    def norm(i, _):
        x = tok[pl.ds(i * blk, blk), :].astype(F32)
        normed[pl.ds(i * blk, blk), :] = (
            x * lax.rsqrt(jnp.mean(x * x, axis=-1, keepdims=True) + 1e-06)).astype(BF16)
        return 0
    lax.fori_loop(0, nblk, norm, 0)

    for c in bank_loads:
        c.wait()

    group = max(g for g in range(1, 6) if (nblk - 1) % g == 0)

    def stage(t, _):
        @pl.when(t < NS - 2)
        def _():
            send_own(t + 2)

        @pl.when(t < NS)
        def _():
            relay(t, 1)

        @pl.when(t > 0)
        def _():
            for o in range(S):
                @pl.when(s != o)
                def _():
                    twin(t - 1, o, 1 - b).wait_recv()
            project(t - 1, 0, steps // 2)

        @pl.when(t < NS)
        def _():
            relay(t, 2)

        @pl.when(t > 0)
        def _():
            project(t - 1, steps // 2, steps)
            last = slots[nblk - 1]

            @pl.when(s < S - 1)
            def _():
                halo_out[t - 1] = kv[last]
                halo(t - 1).start()
            queries(t - 1)

        @pl.when(t < NS)
        def _():
            for d in range(3, S):
                relay(t, d)

        @pl.when(t == 0)
        def _():
            @pl.when(h != s)
            def _():
                wo_turn(s, dev(h, s, b)).wait_recv()
                twin(NS, s, b).start()
            send_own(NS)

        for d in range(1, S):
            @pl.when(t == d)
            def _():
                relay(NS, d)

        @pl.when(t > 0)
        def _():
            u = t - 1

            def some(i, _):
                blocks = []
                for g in range(group):
                    c = 1 + i * group + g
                    at = slots[c - 1]
                    blocks.append((c, lambda k, at=at: kv[at, :, k * CW:(k + 1) * CW]))
                attend(u, None, blocks)
                return 0
            lax.fori_loop(0, (nblk - 1) // group, some, 0)

            @pl.when(s > 0)
            def _():
                halo(u).wait_recv()
            attend(u, None, [(0, lambda k: halo_in[u, :, k * CW:(k + 1) * CW])])
            for k in range(3):
                att_send(u, k).start()
            att_here(u).start()

        return 0

    lax.fori_loop(0, NS + 1, stage, 0)

    for o in range(S):
        @pl.when(jnp.logical_or(s != o, h != s))
        def _():
            twin(NS, o, 1 - b).wait_recv()

    tile = T // 4

    def fold(j, _):
        att_here(j).wait()
        for k in range(3):
            rcopy(att_own.at[j], att.at[j, :, pl.ds(peers[k] * CW, CW)], att_s.at[j, k], att_r.at[j, k],
                  dev(s, peers[k], b)).wait_recv()

        def rows(i, _):
            r = pl.ds(i * tile, tile)
            part = jnp.dot(att[j, r, :], WO[j], preferred_element_type=F32)

            @pl.when(j == 0)
            def _():
                acc[r, :] = part

            @pl.when(jnp.logical_and(j > 0, j < NS - 1))
            def _():
                acc[r, :] += part

            @pl.when(j == NS - 1)
            def _():
                out[r, :] = (acc[r, :] + part).astype(BF16)
            return 0
        lax.fori_loop(0, 4, rows, 0)
        return 0
    lax.fori_loop(0, NS, fold, 0)

    def drain_weights(t):
        for d in range(S):
            @pl.when(jnp.logical_and(s >= d, s < S - 1))
            def _():
                right(t, s - d).wait_send()

            @pl.when(jnp.logical_and(s + d < S, s > 0))
            def _():
                left(t, s + d).wait_send()
        for o in range(S):
            @pl.when(s != o)
            def _():
                twin(t, o, b).wait_send()

    def drain(t, _):
        drain_weights(t)

        @pl.when(s < S - 1)
        def _():
            halo(t).wait_send()
        for k in range(3):
            att_send(t, k).wait_send()
        return 0
    lax.fori_loop(0, NS, drain, 0)
    drain_weights(NS)

    @pl.when(h != s)
    def _():
        twin(NS, s, b).wait_send()
        wo_turn(h, dev(h, s, b)).wait_send()


def one_kernel(tokens, neighbor_bank, slots, w_query, w_key, w_value, w_out):
    S, H = lax.axis_size("seq"), lax.axis_size("head")
    T, D = tokens.shape
    nblk, nrow = neighbor_bank.shape[:2]
    width = w_query.shape[1]
    NS = width // HEAD_DIM
    CW = HEAD_DIM
    out_cols = D // H
    dma = pltpu.SemaphoreType.DMA
    hbm = pl.BlockSpec(memory_space=pl.ANY)
    return pl.pallas_call(
        functools.partial(fused, S, H, NS),
        out_shape=jax.ShapeDtypeStruct((T, out_cols), BF16),
        in_specs=[hbm, hbm, pl.BlockSpec(memory_space=pltpu.SMEM), hbm, hbm, hbm, hbm],
        out_specs=pl.BlockSpec(memory_space=pltpu.VMEM),
        scratch_shapes=[
            pltpu.VMEM((NS, D, 3 * CW), BF16),
            pltpu.VMEM((NS, H * CW, out_cols), BF16),
            pltpu.VMEM((T, D), BF16),
            pltpu.VMEM((T, D), BF16),
            pltpu.VMEM((nblk, nrow, D), BF16),
            pltpu.VMEM((nblk, nrow, 2 * CW), BF16),
            pltpu.VMEM((T, CW), BF16),
            pltpu.VMEM((NS, nrow, 2 * CW), BF16),
            pltpu.VMEM((NS, nrow, 2 * CW), BF16),
            pltpu.VMEM((NS, T, CW), BF16),
            pltpu.VMEM((NS, T, H * CW), BF16),
            pltpu.VMEM((T, out_cols), F32),
            dma((nblk + 1,)),
            dma((3 * NS,)),
            dma((NS + 1, S)), dma((NS + 1, S)), dma((NS + 1, S)), dma((NS + 1, S)), dma((NS + 1, S)),
            dma((NS,)), dma((NS,)),
            dma((NS, 3)), dma((NS, 3)), dma((NS,)),
            dma, dma, dma,
        ],
        compiler_params=pltpu.CompilerParams(
            collective_id=0, has_side_effects=True, vmem_limit_bytes=63 * 1024 * 1024),
    )(tokens, neighbor_bank, slots, w_query, w_key, w_value, w_out.reshape(NS, CW, -1))


def passed_along(block, axis, distance):
    devices = range(lax.axis_size(axis))
    route = [(i - distance, i) for i in devices if i - distance in devices]
    return lax.ppermute(block, axis, route)


def attend(query_blocks, key_blocks, value_blocks):
    scores = jnp.einsum(
        "cmhd,cnhd->chmn", query_blocks, key_blocks, preferred_element_type=jnp.float32
    ) / math.sqrt(HEAD_DIM)
    peak_score = jnp.max(scores, axis=-1, keepdims=True)
    exponent = jnp.exp(scores - peak_score)
    weights = (exponent / jnp.sum(exponent, axis=-1, keepdims=True)).astype(jnp.bfloat16)
    blended = jnp.einsum(
        "chmn,cnhd->cmhd", weights, value_blocks, preferred_element_type=jnp.float32
    ).astype(jnp.bfloat16)
    return blended.reshape(blended.shape[0] * blended.shape[1], blended.shape[2] * blended.shape[3])


def fold_rows(source, shard_rows):
    return jnp.dot(source, shard_rows, preferred_element_type=jnp.float32)


def local(tokens, neighbor_bank, slots, w_query, w_key, w_value, w_out):
    tok_rows, model_width = tokens.shape
    block_count = neighbor_bank.shape[0]
    neighbor_rows = neighbor_bank.shape[1]
    block_len = tok_rows // block_count
    local_width = w_query.shape[1]
    local_heads = local_width // HEAD_DIM
    hidden = tokens.astype(jnp.float32)
    normed = (hidden * lax.rsqrt(jnp.mean(hidden * hidden, axis=-1, keepdims=True) + 1e-06)).astype(
        jnp.bfloat16
    )
    retrieved = jnp.take(neighbor_bank, slots, axis=0)
    arrived = passed_along(retrieved[block_count - 1], "seq", 1)
    context = jnp.concatenate([arrived[None], retrieved[: block_count - 1]], axis=0)
    context_flat = context.reshape(block_count * neighbor_rows, model_width)
    query_sum = fold_rows(normed, lax.all_gather(w_query, "seq", axis=0, tiled=True))
    key_sum = fold_rows(context_flat, lax.all_gather(w_key, "seq", axis=0, tiled=True))
    value_sum = fold_rows(context_flat, lax.all_gather(w_value, "seq", axis=0, tiled=True))
    query_blocks = query_sum.astype(jnp.bfloat16).reshape(
        block_count, block_len, local_heads, HEAD_DIM
    )
    key_blocks = key_sum.astype(jnp.bfloat16).reshape(
        block_count, neighbor_rows, local_heads, HEAD_DIM
    )
    value_blocks = value_sum.astype(jnp.bfloat16).reshape(
        block_count, neighbor_rows, local_heads, HEAD_DIM
    )
    attended = attend(query_blocks, key_blocks, value_blocks)
    every_head = lax.all_gather(attended, "head", axis=1, tiled=True)
    wide_rows = lax.all_gather(w_out, "seq", axis=1, tiled=True)
    own_columns = lax.all_to_all(wide_rows, "head", split_axis=1, concat_axis=0, tiled=True)
    return jnp.dot(every_head, own_columns, preferred_element_type=jnp.float32).astype(jnp.bfloat16)


def solution(mesh):
    in_specs = (
        P(("batch", "seq"), None),
        P(("batch", "seq"), None, None),
        P(("batch", "seq")),
        P("seq", "head"),
        P("seq", "head"),
        P("seq", "head"),
        P("head", "seq"),
    )
    out_specs = P(("batch", "seq"), "head")
    square = mesh.shape["seq"] == 4 and mesh.shape["head"] == 4 and mesh.shape["batch"] == 2
    body = one_kernel if square else local
    return jax.shard_map(body, mesh=mesh, in_specs=in_specs, out_specs=out_specs, check_vma=False)
```

profile of v0, /device:TPU:25, one launch (start us, length us, event | category | flops | bytes accessed | tf_op | source)
XLA Modules:
  0.0 130.5 jit_solution(10294131557726495689)
XLA Ops:
  0.0 128.3 %shard_map.73 = bf16[1024,512]{1,0:T(8,128)(2,1)} custom-call(bf16[1024,2048]{1,0:T(8,128)(2,1)} %tokens.1, bf16[16,256,2048]{2,1,0:T(8,128)(2,1)} %bank.1, s32[16]{0:T(128)} %slots.1, bf16[512,512]{1,0:T(8,128)(2,1)} %w_query.1, bf16[512,512]{1,0:T(8,128)(2,1)} %w_key.1, bf16[512,512]{1,0:T(8,128)(2,1)} %w_value.1, bf16[4,128,512]{2,1,0:T(8,128)(2,1)} %bitcast.1), custom_call_target="tpu_custom_call" | custom-call | tf_op jit(solution)/shard_map/pallas_call | solution.py:335
  128.3 2.3 %copy.9 = bf16[1024,512]{1,0:T(8,128)(2,1)} copy(bf16[1024,512]{1,0:T(8,128)(2,1)} %shard_map.73) | data formatting | bytes 2097152
where the time goes:
time: 131 us
  Pallas kernels  128 us (98%)
  local copies, waits for them, and re-layouts  2.26 us (2%)
    pallas_call x1, Pallas kernels, one_kernel(): pl.pallas_call(functools.partial(fused, S, H, NS), out_shape=jax.ShapeDty...  128 us

commit v1 on v0

v1 whole, which is shorter than its diff:
```python
import functools
import math

import jax
import jax.numpy as jnp
from jax import lax
from jax.experimental import pallas as pl
from jax.experimental.pallas import tpu as pltpu
from jax.sharding import PartitionSpec as P

HEAD_DIM = 128
F32 = jnp.float32
BF16 = jnp.bfloat16


COMM = True
COMP = True


def fused(S, H, NS, per, tokens, bank, slots, w_query, w_key, w_value, w_out, out,
          G, WO, tok, normed, rows_in, halo_out, halo_in, qb, att, acc,
          ld_sem, wl_sem, zr, xr, send_r, send_l, send_x,
          wzr, wxr, wsend_r, wsend_l, wsend_x, turn_s, turn_r, turn_l,
          hz_s, hz_r, hd_s, hd_r, att_s, att_r):
    s, h, b = lax.axis_index("seq"), lax.axis_index("head"), lax.axis_index("batch")
    nblk, nrow, D = bank.shape
    T = tokens.shape[0]
    blk = T // nblk
    CW = HEAD_DIM
    RS = w_query.shape[0]
    RH = RS // 2
    KO = H * CW
    KH = KO // 2
    KQ = KH // 2
    NW = 2 * NS
    groups = nblk // per
    GR = per * blk
    HR = nrow // 2

    def dev(seq, head, batch):
        return {"seq": seq, "head": head, "batch": batch}

    def rcopy(src, dst, ss, rs, device):
        return pltpu.make_async_remote_copy(
            src_ref=src, dst_ref=dst, send_sem=ss, recv_sem=rs,
            device_id=device, device_id_type=pl.DeviceIdType.MESH)

    w_loads = []
    for j in range(NS):
        for k, w in enumerate((w_query, w_key, w_value)):
            c = pltpu.make_async_copy(
                w.at[:, pl.ds(j * CW, CW)],
                G.at[j, pl.ds(s * RS, RS), pl.ds(k * CW, CW)], wl_sem.at[k * NS + j])
            c.start()
            w_loads.append(c)
    wo_own = pltpu.make_async_copy(w_out, WO.at[:, pl.ds(h * CW, CW), :], turn_l)

    @pl.when(h == s)
    def _():
        wo_own.start()
    tok_load = pltpu.make_async_copy(tokens, tok, ld_sem.at[nblk])
    tok_load.start()
    bank_loads = [pltpu.make_async_copy(bank.at[i], rows_in.at[i], ld_sem.at[i]) for i in range(nblk)]
    for c in bank_loads:
        c.start()

    barrier = pltpu.get_barrier_semaphore()
    for i in range(S):
        for k in range(H):
            @pl.when(jnp.logical_or(s != i, h != k))
            def _():
                pl.semaphore_signal(barrier, inc=1, device_id=dev(i, k, b), device_id_type=pl.DeviceIdType.MESH)
    pl.semaphore_signal(barrier, inc=1, device_id=dev(s, h, 1 - b), device_id_type=pl.DeviceIdType.MESH)
    pl.semaphore_wait(barrier, S * H)

    def chunk(t, origin, half):
        return G.at[t, pl.ds(origin * RS + half * RH, RH), :]

    edge = jnp.logical_or(s == 0, s == S - 1)
    middle = jnp.logical_and(s > 0, s < S - 1)
    near_dev = (s - 1) * 3
    far_dev = 3 - s
    edge_dev = 1 + s // 3

    def near(t, origin):
        return rcopy(chunk(t, origin, b), chunk(t, origin, b), send_r.at[t, origin], zr.at[t, origin],
                     dev(near_dev, h, b))

    def far(t, origin):
        return rcopy(chunk(t, origin, b), chunk(t, origin, b), send_l.at[t, origin], zr.at[t, origin],
                     dev(far_dev, h, b))

    def inward(t):
        return rcopy(chunk(t, s, b), chunk(t, s, b), send_r.at[t, s], zr.at[t, s], dev(edge_dev, h, b))

    def twin(t, origin, half):
        return rcopy(chunk(t, origin, half), chunk(t, origin, half), send_x.at[t, origin], xr.at[t, origin],
                     dev(s, h, 1 - b))

    def edge_event(t, d):
        o = d + (s // 3) * (3 - 2 * d)
        inward_from(t, o).wait_recv()
        twin(t, o, b).start()

    def inward_from(t, o):
        return rcopy(chunk(t, o, b), chunk(t, o, b), send_r.at[t, o], zr.at[t, o], dev(edge_dev, h, b))

    def mid_first(t):
        a, e = 3 - s, 3 * (s - 1)
        far(t, a).wait_recv()
        near(t, a).start()
        twin(t, a, b).start()
        far(t, e).wait_recv()
        far(t, e).start()
        twin(t, e, b).start()

    def mid_second(t):
        o = 3 * (2 - s)
        near(t, o).wait_recv()
        near(t, o).start()
        twin(t, o, b).start()

    def turn(j, device):
        return rcopy(w_out, WO.at[:, pl.ds(j * CW, CW), :], turn_s, turn_r.at[j], device)

    def wpart(k, half):
        return WO.at[k // 2, pl.ds(half * KH + (k % 2) * KQ, KQ), :]

    def wright(k):
        return rcopy(wpart(k, b), wpart(k, b), wsend_r.at[k], wzr.at[k], dev(lax.rem(s + 1, S), h, b))

    def wleft(k):
        return rcopy(wpart(k, b), wpart(k, b), wsend_l.at[k], wzr.at[k], dev(lax.rem(s + S - 1, S), h, b))

    def wtwin(k, half):
        return rcopy(wpart(k, half), wpart(k, half), wsend_x.at[k], wxr.at[k], dev(s, h, 1 - b))

    def wo_turned():
        wo_own.wait()
        for j in range(H):
            @pl.when(j != h)
            def _():
                turn(j, dev(s, s, b)).wait_recv()

    def wo_out(rightward):
        for k in range(NW):
            @pl.when(jnp.logical_and(rightward, s < S - 1))
            def _():
                wright(k).start()

            @pl.when(jnp.logical_and(jnp.logical_not(rightward), s > 0))
            def _():
                wleft(k).start()

    def wrelay(k):
        wright(k).wait_recv()

        @pl.when(jnp.logical_and(s > h, s < S - 1))
        def _():
            wright(k).start()

        @pl.when(jnp.logical_and(s < h, s > 0))
        def _():
            wleft(k).start()
        wtwin(k, b).start()

    side = lax.rem(h, 2)
    lead = h >= H // 2
    mate = (h // 2) * 2 + 1 - side
    peers = (mate, lax.rem(h + 2, H), lax.rem(mate + 2, H))

    def halo_z():
        return rcopy(halo_out, halo_in.at[pl.ds(side * HR, HR)], hz_s, hz_r, dev(lax.rem(s + 1, S), h, b))

    def halo_across():
        part = halo_in.at[pl.ds(side * HR, HR)]
        return rcopy(part, part, hd_s.at[0], hd_r.at[0], dev(s, lax.rem(h + 2, H), b))

    def halo_mate(half):
        part = halo_in.at[pl.ds(half * HR, HR)]
        return rcopy(part, part, hd_s.at[1], hd_r.at[1], dev(s, mate, b))

    def halo_spread():
        @pl.when(jnp.logical_and(lead, s > 0))
        def _():
            halo_z().wait_recv()
            halo_across().start()
            halo_mate(side).start()

    def halo_pass():
        @pl.when(jnp.logical_and(jnp.logical_not(lead), s > 0))
        def _():
            halo_across().wait_recv()
            halo_mate(side).start()

    def halo_take():
        @pl.when(s > 0)
        def _():
            halo_mate(1 - side).wait_recv()
            rows_in[nblk] = halo_in[...]

    def att_send(t, g, k):
        part = att.at[t, h, pl.ds(g * GR, GR), :]
        return rcopy(part, part, att_s.at[t, g, k], att_r.at[t, g, k], dev(s, peers[k], b))

    def att_wait(t, g, k):
        part = att.at[t, peers[k], pl.ds(g * GR, GR), :]
        return rcopy(part, part, att_s.at[t, g, k], att_r.at[t, g, k], dev(s, peers[k], b))

    scale = math.log2(math.e) / math.sqrt(HEAD_DIM)

    def unit(t, g):
        if COMP:
            rows = []
            for i in range(per):
                c = g * per + i
                at = slots[jnp.maximum(c - 1, 0)]
                rows.append(rows_in[jnp.where(c == 0, nblk, at)])
            kv = jnp.dot(jnp.concatenate(rows, axis=0), G[t, :, pl.ds(CW, 2 * CW)],
                         preferred_element_type=F32).astype(BF16)
            scores = []
            for i in range(per):
                q = qb[lax.rem(t, 2), pl.ds((g * per + i) * blk, blk), :]
                scores.append(lax.dot_general(q, kv[i * nrow:(i + 1) * nrow, :CW], (((1,), (1,)), ((), ())),
                                              preferred_element_type=F32))
            for i in range(per):
                e = jnp.exp2((scores[i] - jnp.max(scores[i], axis=-1, keepdims=True)) * scale)
                p = (e * (1.0 / jnp.sum(e, axis=-1, keepdims=True))).astype(BF16)
                o = jnp.dot(p, kv[i * nrow:(i + 1) * nrow, CW:], preferred_element_type=F32)
                att[t, h, pl.ds((g * per + i) * blk, blk), :] = o.astype(BF16)
        if COMM:
            for k in range(3):
                att_send(t, g, k).start()

    def queries(t):
        if COMP:
            qb[lax.rem(t, 2)] = jnp.dot(normed[...], G[t, :, pl.ds(0, CW)], preferred_element_type=F32).astype(BF16)

    def loaded(j):
        for c in w_loads[3 * j:3 * j + 3]:
            c.wait()

    loaded(0)
    if COMM:
        @pl.when(middle)
        def _():
            near(0, s).start()
            far(0, s).start()

        @pl.when(edge)
        def _():
            inward(0).start()
    loaded(1)
    if COMM:
        @pl.when(middle)
        def _():
            near(1, s).start()

        @pl.when(edge)
        def _():
            inward(1).start()

        @pl.when(h != s)
        def _():
            turn(h, dev(s, s, b)).start()
    loaded(2)
    loaded(3)
    if COMM:
        @pl.when(edge)
        def _():
            inward(2).start()
            inward(3).start()

    @pl.when(s == 0)
    def _():
        rows_in[nblk] = jnp.zeros((nrow, D), BF16)

    for c in bank_loads:
        c.wait()
    if COMM:
        @pl.when(jnp.logical_and(lead, s < S - 1))
        def _():
            halo_out[...] = rows_in[slots[nblk - 1], pl.ds(side * HR, HR), :]
            halo_z().start()

    tok_load.wait()

    def norm(i, _):
        x = tok[pl.ds(i * blk, blk), :].astype(F32)
        normed[pl.ds(i * blk, blk), :] = (
            x * lax.rsqrt(jnp.mean(x * x, axis=-1, keepdims=True) + 1e-06)).astype(BF16)
        return 0
    if COMP:
        lax.fori_loop(0, nblk, norm, 0)

    def first_edge():
        for t, d in ((0, 1), (1, 1), (0, 2), (0, 3), (2, 1)):
            edge_event(t, d)

        @pl.when(h == s)
        def _():
            wo_turned()
            wo_out(s == 0)

    def first_mid():
        mid_first(0)
        far(1, s).start()
        mid_second(0)
        near(2, s).start()
        mid_first(1)
        far(2, s).start()
        mid_second(1)
        near(3, s).start()

    edge_plan = {0: ((1, 2),), 1: ((1, 3),), 3: ((3, 1),), 4: ((2, 2),), 5: ((2, 3),), 7: ((3, 2),), 8: ((3, 3),)}
    edge_w = {10: (0,), 11: (1,), 12: (2, 3), 13: (4,), 14: (5,), 15: (6,), 16: (7,)}
    early_w = {4: (0, 1), 5: (2, 3), 6: (4, 5), 7: (6, 7)}
    late_w = {7: (0, 1), 8: (2, 3), 9: (4,), 10: (5,), 11: (6,), 12: (7,)}

    def events(n):
        @pl.when(edge)
        def _():
            for at, evs in edge_plan.items():
                @pl.when(n == at)
                def _():
                    for e in evs:
                        edge_event(*e)

            @pl.when(h != s)
            def _():
                for at, ks in edge_w.items():
                    @pl.when(n == at)
                    def _():
                        for k in ks:
                            wrelay(k)

        @pl.when(n == 0)
        def _():
            halo_spread()

        @pl.when(n == 5)
        def _():
            halo_pass()

        @pl.when(middle)
        def _():
            @pl.when(n == 0)
            def _():
                mid_first(2)
                far(3, s).start()

            @pl.when(n == 1)
            def _():
                mid_second(2)

            @pl.when(n == 3)
            def _():
                mid_first(3)

                @pl.when(h == s)
                def _():
                    wo_turned()
                    wo_out(s == 1)

            @pl.when(n == 4)
            def _():
                mid_second(3)

                @pl.when(h == s)
                def _():
                    wo_out(s == 2)

            @pl.when(h == near_dev)
            def _():
                for at, ks in early_w.items():
                    @pl.when(n == at)
                    def _():
                        for k in ks:
                            wrelay(k)

            @pl.when(jnp.logical_and(h != near_dev, h != s))
            def _():
                for at, ks in late_w.items():
                    @pl.when(n == at)
                    def _():
                        for k in ks:
                            wrelay(k)

    if COMM:
        @pl.when(edge)
        def _():
            first_edge()

        @pl.when(middle)
        def _():
            first_mid()

    def slot(n, _):
        t, gi = n // groups, lax.rem(n, groups)

        @pl.when(jnp.logical_and(gi == 0, t < NS))
        def _():
            if COMM:
                for o in range(S):
                    @pl.when(s != o)
                    def _():
                        twin(t, o, 1 - b).wait_recv()
            queries(t)

        @pl.when(n == 2 * groups - 1)
        def _():
            if COMM:
                halo_take()
        last = jnp.logical_or(gi == groups - 1, t == NS)
        u = jnp.where(last, t - 1, t)

        @pl.when(u >= 0)
        def _():
            unit(u, jnp.where(last, 0, gi + 1))
        if COMM:
            events(n)
        return 0

    lax.fori_loop(0, NS * groups + 1, slot, 0)

    tile = T // 4

    def fold(j, _):
        if COMM:
            @pl.when(h != s)
            def _():
                for k in range(2):
                    wtwin(2 * j + k, 1 - b).wait_recv()

            def arrived(g, _):
                for k in range(3):
                    att_wait(j, g, k).wait_recv()
                return 0
            lax.fori_loop(0, groups, arrived, 0)

        def rows(i, _):
            r = pl.ds(i * tile, tile)
            part = jnp.dot(jnp.concatenate([att[j, k, r, :] for k in range(H)], axis=1), WO[j],
                           preferred_element_type=F32)

            @pl.when(j == 0)
            def _():
                acc[r, :] = part

            @pl.when(jnp.logical_and(j > 0, j < NS - 1))
            def _():
                acc[r, :] += part

            @pl.when(j == NS - 1)
            def _():
                out[r, :] = (acc[r, :] + part).astype(BF16)
            return 0
        if COMP:
            lax.fori_loop(0, 4, rows, 0)
        return 0
    lax.fori_loop(0, NS, fold, 0)

    def drain(t, _):
        @pl.when(edge)
        def _():
            inward(t).wait_send()

        @pl.when(middle)
        def _():
            for o in (s, 3 - s, 3 * (2 - s)):
                near(t, o).wait_send()
            for o in (s, 3 * (s - 1)):
                far(t, o).wait_send()
        for o in range(S):
            @pl.when(s != o)
            def _():
                twin(t, o, b).wait_send()

        def sent(g, _):
            for k in range(3):
                att_send(t, g, k).wait_send()
            return 0
        lax.fori_loop(0, groups, sent, 0)

        for k in (2 * t, 2 * t + 1):
            @pl.when(jnp.logical_and(s >= h, s < S - 1))
            def _():
                wright(k).wait_send()

            @pl.when(jnp.logical_and(s <= h, s > 0))
            def _():
                wleft(k).wait_send()

            @pl.when(h != s)
            def _():
                wtwin(k, b).wait_send()
        return 0
    if COMM:
        lax.fori_loop(0, NS, drain, 0)

        @pl.when(h != s)
        def _():
            turn(h, dev(s, s, b)).wait_send()

        @pl.when(jnp.logical_and(lead, s < S - 1))
        def _():
            halo_z().wait_send()

        @pl.when(s > 0)
        def _():
            halo_mate(side).wait_send()

            @pl.when(lead)
            def _():
                halo_across().wait_send()
    else:
        @pl.when(h == s)
        def _():
            wo_own.wait()


def one_kernel(tokens, neighbor_bank, slots, w_query, w_key, w_value, w_out):
    S, H = lax.axis_size("seq"), lax.axis_size("head")
    T, D = tokens.shape
    nblk, nrow = neighbor_bank.shape[:2]
    width = w_query.shape[1]
    NS = width // HEAD_DIM
    CW = HEAD_DIM
    out_cols = D // H
    per = nblk // 4
    groups = nblk // per
    dma = pltpu.SemaphoreType.DMA
    hbm = pl.BlockSpec(memory_space=pl.ANY)
    return pl.pallas_call(
        functools.partial(fused, S, H, NS, per),
        out_shape=jax.ShapeDtypeStruct((T, out_cols), BF16),
        in_specs=[hbm, hbm, pl.BlockSpec(memory_space=pltpu.SMEM), hbm, hbm, hbm, hbm],
        out_specs=pl.BlockSpec(memory_space=pltpu.VMEM),
        scratch_shapes=[
            pltpu.VMEM((NS, D, 3 * CW), BF16),
            pltpu.VMEM((NS, H * CW, out_cols), BF16),
            pltpu.VMEM((T, D), BF16),
            pltpu.VMEM((T, D), BF16),
            pltpu.VMEM((nblk + 1, nrow, D), BF16),
            pltpu.VMEM((nrow // 2, D), BF16),
            pltpu.VMEM((nrow, D), BF16),
            pltpu.VMEM((2, T, CW), BF16),
            pltpu.VMEM((NS, H, T, CW), BF16),
            pltpu.VMEM((T, out_cols), F32),
            dma((nblk + 1,)),
            dma((3 * NS,)),
            dma((NS, S)), dma((NS, S)), dma((NS, S)), dma((NS, S)), dma((NS, S)),
            dma((2 * NS,)), dma((2 * NS,)), dma((2 * NS,)), dma((2 * NS,)), dma((2 * NS,)), dma, dma((H,)), dma,
            dma, dma, dma((2,)), dma((2,)),
            dma((NS, groups, 3)), dma((NS, groups, 3)),
        ],
        compiler_params=pltpu.CompilerParams(
            collective_id=0, has_side_effects=True, vmem_limit_bytes=63 * 1024 * 1024),
    )(tokens, neighbor_bank, slots, w_query, w_key, w_value, w_out.reshape(NS, CW, -1))


def passed_along(block, axis, distance):
    devices = range(lax.axis_size(axis))
    route = [(i - distance, i) for i in devices if i - distance in devices]
    return lax.ppermute(block, axis, route)


def attend(query_blocks, key_blocks, value_blocks):
    scores = jnp.einsum(
        "cmhd,cnhd->chmn", query_blocks, key_blocks, preferred_element_type=jnp.float32
    ) / math.sqrt(HEAD_DIM)
    peak_score = jnp.max(scores, axis=-1, keepdims=True)
    exponent = jnp.exp(scores - peak_score)
    weights = (exponent / jnp.sum(exponent, axis=-1, keepdims=True)).astype(jnp.bfloat16)
    blended = jnp.einsum(
        "chmn,cnhd->cmhd", weights, value_blocks, preferred_element_type=jnp.float32
    ).astype(jnp.bfloat16)
    return blended.reshape(blended.shape[0] * blended.shape[1], blended.shape[2] * blended.shape[3])


def fold_rows(source, shard_rows):
    return jnp.dot(source, shard_rows, preferred_element_type=jnp.float32)


def local(tokens, neighbor_bank, slots, w_query, w_key, w_value, w_out):
    tok_rows, model_width = tokens.shape
    block_count = neighbor_bank.shape[0]
    neighbor_rows = neighbor_bank.shape[1]
    block_len = tok_rows // block_count
    local_width = w_query.shape[1]
    local_heads = local_width // HEAD_DIM
    hidden = tokens.astype(jnp.float32)
    normed = (hidden * lax.rsqrt(jnp.mean(hidden * hidden, axis=-1, keepdims=True) + 1e-06)).astype(
        jnp.bfloat16
    )
    retrieved = jnp.take(neighbor_bank, slots, axis=0)
    arrived = passed_along(retrieved[block_count - 1], "seq", 1)
    context = jnp.concatenate([arrived[None], retrieved[: block_count - 1]], axis=0)
    context_flat = context.reshape(block_count * neighbor_rows, model_width)
    query_sum = fold_rows(normed, lax.all_gather(w_query, "seq", axis=0, tiled=True))
    key_sum = fold_rows(context_flat, lax.all_gather(w_key, "seq", axis=0, tiled=True))
    value_sum = fold_rows(context_flat, lax.all_gather(w_value, "seq", axis=0, tiled=True))
    query_blocks = query_sum.astype(jnp.bfloat16).reshape(
        block_count, block_len, local_heads, HEAD_DIM
    )
    key_blocks = key_sum.astype(jnp.bfloat16).reshape(
        block_count, neighbor_rows, local_heads, HEAD_DIM
    )
    value_blocks = value_sum.astype(jnp.bfloat16).reshape(
        block_count, neighbor_rows, local_heads, HEAD_DIM
    )
    attended = attend(query_blocks, key_blocks, value_blocks)
    every_head = lax.all_gather(attended, "head", axis=1, tiled=True)
    wide_rows = lax.all_gather(w_out, "seq", axis=1, tiled=True)
    own_columns = lax.all_to_all(wide_rows, "head", split_axis=1, concat_axis=0, tiled=True)
    return jnp.dot(every_head, own_columns, preferred_element_type=jnp.float32).astype(jnp.bfloat16)


def solution(mesh):
    in_specs = (
        P(("batch", "seq"), None),
        P(("batch", "seq"), None, None),
        P(("batch", "seq")),
        P("seq", "head"),
        P("seq", "head"),
        P("seq", "head"),
        P("head", "seq"),
    )
    out_specs = P(("batch", "seq"), "head")
    square = mesh.shape["seq"] == 4 and mesh.shape["head"] == 4 and mesh.shape["batch"] == 2
    body = one_kernel if square else local
    return jax.shard_map(body, mesh=mesh, in_specs=in_specs, out_specs=out_specs, check_vma=False)
```

time: 131 us -> 107 us (0.82)
  Pallas kernels: 128 us -> 105 us
    pallas_call x1, Pallas kernels: 128 us -> 105 us  [one_kernel(): pl.pallas_call(functools.partial(fused, S, H, NS, per), out_shape=jax.Sha...]
where the time goes in v1:
time: 107 us
  Pallas kernels  105 us (98%)
  local copies, waits for them, and re-layouts  2.26 us (2%)
    pallas_call x1, Pallas kernels, one_kernel(): pl.pallas_call(functools.partial(fused, S, H, NS, per), out_shape=jax.Sha...  105 us
    unnamed x1, local copies, waits for them, and re-layouts  2.26 us

profile of v1, /device:TPU:25, one launch (start us, length us, event | category | flops | bytes accessed | tf_op | source)
XLA Modules:
  0.0 106.9 jit_solution(7882438665511594617)
XLA Ops:
  0.0 104.6 %shard_map.73 = bf16[1024,512]{1,0:T(8,128)(2,1)} custom-call(bf16[1024,2048]{1,0:T(8,128)(2,1)} %tokens.1, bf16[16,256,2048]{2,1,0:T(8,128)(2,1)} %bank.1, s32[16]{0:T(128)} %slots.1, bf16[512,512]{1,0:T(8,128)(2,1)} %w_query.1, bf16[512,512]{1,0:T(8,128)(2,1)} %w_key.1, bf16[512,512]{1,0:T(8,128)(2,1)} %w_value.1, bf16[4,128,512]{2,1,0:T(8,128)(2,1)} %bitcast.1), custom_call_target="tpu_custom_call" | custom-call | tf_op jit(solution)/shard_map/pallas_call | solution.py:534
  104.6 2.3 %copy.9 = bf16[1024,512]{1,0:T(8,128)(2,1)} copy(bf16[1024,512]{1,0:T(8,128)(2,1)} %shard_map.73) | data formatting | bytes 2097152

commit v2 on v1

v2 whole, which is shorter than its diff:
```python
import functools
import math

import jax
import jax.numpy as jnp
from jax import lax
from jax.experimental import pallas as pl
from jax.experimental.pallas import tpu as pltpu
from jax.sharding import PartitionSpec as P

HEAD_DIM = 128
F32 = jnp.float32
BF16 = jnp.bfloat16


NZ, NX = 9, 7
HALO_FIRST = 2
EDGE_QKV = {0: ((1, 2),), 1: ((1, 3),), 2: ((2, 2),), 3: ((2, 3),), 4: ((3, 1),), 5: ((3, 2),), 6: ((3, 3),)}
EDGE_W = {7: (0,), 8: (1,), 9: (2,), 10: (3,), 11: (4,)}
EDGE_W_LATE = {9: (0, 1), 10: (2,), 11: (3, 4)}
EDGE_W_TAIL = ((5,), (), (6,), (7, 8))
VMEM_MIB = 48
MID_W_EARLY = {2: (0, 1), 3: (2, 3), 4: (4, 5), 5: (6, 7, 8)}
MID_W = {5: (0, 1), 6: (2, 3, 4), 7: (5,), 8: (6,), 9: (7, 8)}
HALO_SPREAD = {5: (0, 1), 8: (2, 3)}
HALO_PASS = {8: (0,), 9: (1,), 12: (2, 3)}
COMM = True
COMP = True


def fused(S, H, NS, tokens, bank, slots, w_query, w_key, w_value, w_out, out,
          G, WO, tok, normed, rows_in, halo_out, halo_in, qb, att, acc,
          ld_sem, wl_sem, zr, xr, send_n, send_f, send_x,
          wzr, wxr, wsend_r, wsend_l, wsend_x, turn_s, turn_r, turn_l,
          hz_s, hz_r, hy_s, hy_r, hm_s, hm_r, att_s, att_y, att_m, att_b):
    s, h, b = lax.axis_index("seq"), lax.axis_index("head"), lax.axis_index("batch")
    nblk, nrow, D = bank.shape
    T = tokens.shape[0]
    blk = T // nblk
    CW = HEAD_DIM
    RS = w_query.shape[0]
    RH = RS // 2
    KH = H * CW // 2
    KQ = KH // 2
    NW = 2 * NS
    units = 3
    per = (nblk - 1) // units
    GR = per * blk
    HR = nrow // 2
    HP = HR // NS

    def dev(seq, head, batch):
        return {"seq": seq, "head": head, "batch": batch}

    def rcopy(src, dst, ss, rs, device):
        return pltpu.make_async_remote_copy(
            src_ref=src, dst_ref=dst, send_sem=ss, recv_sem=rs,
            device_id=device, device_id_type=pl.DeviceIdType.MESH)

    edge = jnp.logical_or(s == 0, s == S - 1)
    middle = jnp.logical_and(s > 0, s < S - 1)
    near_dev = (s - 1) * 3
    far_dev = 3 - s
    edge_dev = 1 + s // 3
    side = lax.rem(h, 2)
    lead = h >= H // 2
    mate = (h // 2) * 2 + 1 - side
    across = lax.rem(h + 2, H)
    peers = (mate, across, lax.rem(mate + 2, H))

    w_loads = []
    for j in range(NS):
        for k, w in enumerate((w_query, w_key, w_value)):
            c = pltpu.make_async_copy(
                w.at[:, pl.ds(j * CW, CW)],
                G.at[j, pl.ds(s * RS, RS), pl.ds(k * CW, CW)], wl_sem.at[j])
            w_loads.append(c)
    for c in w_loads[:3]:
        c.start()
    wo_own = pltpu.make_async_copy(w_out, WO.at[:, pl.ds(h * CW, CW), :], turn_l)

    tok_load = pltpu.make_async_copy(tokens, tok, ld_sem.at[1])
    bank_loads = [pltpu.make_async_copy(bank.at[i], rows_in.at[i], ld_sem.at[0]) for i in range(nblk)]

    barrier = pltpu.get_barrier_semaphore()

    def greet(device):
        pl.semaphore_signal(barrier, inc=1, device_id=device, device_id_type=pl.DeviceIdType.MESH)

    for p in peers:
        greet(dev(s, p, b))
    greet(dev(s, h, 1 - b))

    @pl.when(edge)
    def _():
        greet(dev(edge_dev, h, b))
        pl.semaphore_wait(barrier, 5)

    @pl.when(middle)
    def _():
        greet(dev(near_dev, h, b))
        greet(dev(far_dev, h, b))
        pl.semaphore_wait(barrier, 6)

    def chunk(t, origin, half):
        return G.at[t, pl.ds(origin * RS + half * RH, RH), :]

    def near(t, origin):
        return rcopy(chunk(t, origin, b), chunk(t, origin, b), send_n, zr.at[t, origin],
                     dev(near_dev, h, b))

    def far(t, origin):
        return rcopy(chunk(t, origin, b), chunk(t, origin, b), send_f, zr.at[t, origin],
                     dev(far_dev, h, b))

    def inward(t, origin):
        return rcopy(chunk(t, origin, b), chunk(t, origin, b), send_n, zr.at[t, origin],
                     dev(edge_dev, h, b))

    def twin(t, origin, half):
        return rcopy(chunk(t, origin, half), chunk(t, origin, half), send_x, xr.at[t],
                     dev(s, h, 1 - b))

    def edge_event(t, d):
        o = d + (s // 3) * (3 - 2 * d)
        inward(t, o).wait_recv()
        twin(t, o, b).start()

    def mid_first(t):
        a, e = 3 - s, 3 * (s - 1)

        def outer():
            far(t, e).wait_recv()
            far(t, e).start()
            twin(t, e, b).start()
        if t > 0:
            outer()
        far(t, a).wait_recv()
        near(t, a).start()
        twin(t, a, b).start()
        if t == 0:
            outer()

    def mid_second(t):
        o = 3 * (2 - s)
        near(t, o).wait_recv()
        near(t, o).start()
        twin(t, o, b).start()

    def turn(j, device):
        return rcopy(w_out, WO.at[:, pl.ds(j * CW, CW), :], turn_s, turn_r, device)

    def wpart(k, half):
        return WO.at[k // 2, pl.ds(half * KH + (k % 2) * KQ, KQ), :]

    def wpiece(k):
        return wpart(k, b) if k < NW else wpart(2 * NW - 1 - k, 1 - b)

    def wright(k):
        return rcopy(wpiece(k), wpiece(k), wsend_r, wzr.at[k], dev(lax.rem(s + 1, S), h, b))

    def wleft(k):
        return rcopy(wpiece(k), wpiece(k), wsend_l, wzr.at[k], dev(lax.rem(s + S - 1, S), h, b))

    def wtwin(k, half):
        return rcopy(wpart(k, half), wpart(k, half), wsend_x, wxr.at[k // (NX - 1)], dev(s, h, 1 - b))

    def wo_turned():
        wo_own.wait()
        three = WO.at[:, pl.ds(0, (H - 1) * CW), :]
        rcopy(three, three, turn_s, turn_r, dev(s, mate, b)).wait_recv()

    def wo_out(rightward):
        for k in range(NZ):
            @pl.when(jnp.logical_and(rightward, s < S - 1))
            def _():
                wright(k).start()

            @pl.when(jnp.logical_and(jnp.logical_not(rightward), s > 0))
            def _():
                wleft(k).start()

    def wrelay(k):
        wright(k).wait_recv()

        @pl.when(jnp.logical_and(s > h, s < S - 1))
        def _():
            wright(k).start()

        @pl.when(jnp.logical_and(s < h, s > 0))
        def _():
            wleft(k).start()
        if k < NX:
            wtwin(k, b).start()

    def halo_part(p, who):
        return halo_in.at[pl.ds(who * HR + p * HP, HP)]

    def halo_z(p):
        return rcopy(halo_out.at[pl.ds(p * HP, HP)], halo_part(p, side), hz_s, hz_r.at[p],
                     dev(lax.rem(s + 1, S), h, b))

    def halo_y(p):
        return rcopy(halo_part(p, side), halo_part(p, side), hy_s, hy_r.at[p], dev(s, across, b))

    def halo_m(p, who):
        return rcopy(halo_part(p, who), halo_part(p, who), hm_s, hm_r, dev(s, mate, b))

    def halo_spread(p):
        @pl.when(jnp.logical_and(lead, s > 0))
        def _():
            halo_z(p).wait_recv()
            halo_y(p).start()
            halo_m(p, side).start()

    def halo_pass(p):
        @pl.when(jnp.logical_and(jnp.logical_not(lead), s > 0))
        def _():
            halo_y(p).wait_recv()
            halo_m(p, side).start()

    def att_rows(t, who, g):
        if isinstance(g, int) and g == units:
            return att.at[t, who, pl.ds(0, blk), :]
        return att.at[t, who, pl.ds(blk + g * GR, GR), :]

    def att_copy(t, g, who, rs, device):
        return rcopy(att_rows(t, who, g), att_rows(t, who, g), att_s, rs, dev(s, device, b))

    def att_send(t, g):
        att_copy(t, g, h, att_m.at[0, t], mate).start()
        att_copy(t, g, h, att_y.at[t, g], across).start()

    def att_pass(t, g):
        att_copy(t, g, across, att_y.at[t, g], across).wait_recv()
        att_copy(t, g, across, att_m.at[1, t], mate).start()

    def att_got(t):
        for k in range(2):
            block = att.at[t, 0, pl.ds(blk, T - blk), :]
            rcopy(block, block, att_s, att_m.at[k, t], dev(s, mate, b)).wait_recv()

    def att_first(k, device):
        part = att.at[:, h, pl.ds(0, blk), :]
        return rcopy(part, part, att_s, att_b.at[k], dev(s, device, b))

    scale = math.log2(math.e) / math.sqrt(HEAD_DIM)

    def attend_all(blocks):
        scores = []
        for t, c, kv in blocks:
            q = qb[t, pl.ds(c * blk, blk), :]
            scores.append(lax.dot_general(q, kv[:, :CW], (((1,), (1,)), ((), ())), preferred_element_type=F32))
        for (t, c, kv), sc in zip(blocks, scores):
            e = jnp.exp2((sc - jnp.max(sc, axis=-1, keepdims=True)) * scale)
            p = (e * (1.0 / jnp.sum(e, axis=-1, keepdims=True))).astype(BF16)
            o = jnp.dot(p, kv[:, CW:], preferred_element_type=F32)
            att[t, h, pl.ds(c * blk, blk), :] = o.astype(BF16)

    def project(t, rows):
        return jnp.dot(rows, G[t, :, pl.ds(CW, 2 * CW)], preferred_element_type=F32).astype(BF16)

    def unit(t, g):
        first = 1 + g * per
        rows = [rows_in[slots[first + i - 1]] for i in range(per)]
        kv = project(t, jnp.concatenate(rows, axis=0))
        attend_all([(t, first + i, kv[i * nrow:(i + 1) * nrow]) for i in range(per)])

    def queries(t):
        qb[t] = jnp.dot(normed[...], G[t, :, pl.ds(0, CW)], preferred_element_type=F32).astype(BF16)

    def loaded(j):
        own = G.at[j, pl.ds(s * RS, RS), :]
        pltpu.make_async_copy(own, own, wl_sem.at[j]).wait()

    loaded(0)
    for c in w_loads[3:]:
        c.start()
    if COMM:
        @pl.when(middle)
        def _():
            near(0, s).start()
            far(0, s).start()

        @pl.when(edge)
        def _():
            inward(0, s).start()
    loaded(1)
    tok_load.start()

    @pl.when(h == s)
    def _():
        wo_own.start()
    for c in bank_loads:
        c.start()
    if COMM:
        @pl.when(middle)
        def _():
            near(1, s).start()

        @pl.when(edge)
        def _():
            inward(1, s).start()

        @pl.when(h != s)
        def _():
            turn(h, dev(s, s, b)).start()
    loaded(2)
    loaded(3)
    if COMM:
        @pl.when(edge)
        def _():
            inward(2, s).start()
            inward(3, s).start()

            edge_event(0, 1)

        @pl.when(middle)
        def _():
            mid_first(0)
            far(1, s).start()
    tok_load.wait()

    def norm(i, _):
        x = tok[pl.ds(i * blk, blk), :].astype(F32)
        normed[pl.ds(i * blk, blk), :] = (
            x * lax.rsqrt(jnp.mean(x * x, axis=-1, keepdims=True) + 1e-06)).astype(BF16)
        return 0
    if COMP:
        lax.fori_loop(0, nblk, norm, 0)

    pltpu.make_async_copy(bank, rows_in, ld_sem.at[0]).wait()
    if COMM:
        @pl.when(jnp.logical_and(lead, s < S - 1))
        def _():
            halo_out[...] = rows_in[slots[nblk - 1], pl.ds(side * HR, HR), :]

        @pl.when(s == 0)
        def _():
            halo_in[...] = jnp.zeros_like(halo_in)

        @pl.when(edge)
        def _():
            for t, d in ((1, 1), (0, 2), (0, 3), (2, 1)):
                edge_event(t, d)

            @pl.when(h == s)
            def _():
                wo_turned()
                wo_out(s == 0)

        @pl.when(middle)
        def _():
            mid_second(0)
            near(2, s).start()
            mid_first(1)
            far(2, s).start()
            mid_second(1)

    def halo_out_pieces(pieces):
        @pl.when(jnp.logical_and(lead, s < S - 1))
        def _():
            for p in pieces:
                halo_z(p).start()

    def plan(n, table, event):
        for at, items in table.items():
            @pl.when(n == at)
            def _():
                for item in items:
                    event(item)

    def events(n):
        @pl.when(edge)
        def _():
            plan(n, EDGE_QKV, lambda e: edge_event(*e))

            late = jnp.logical_and(s == S - 1, lead)

            @pl.when(jnp.logical_and(h != s, jnp.logical_not(late)))
            def _():
                plan(n, EDGE_W, wrelay)

            @pl.when(jnp.logical_and(h != s, late))
            def _():
                plan(n, EDGE_W_LATE, wrelay)

        @pl.when(middle)
        def _():
            @pl.when(n == 0)
            def _():
                mid_first(2)
                far(3, s).start()

            @pl.when(n == 1)
            def _():
                mid_second(2)

        @pl.when(n == 1)
        def _():
            halo_out_pieces(range(HALO_FIRST))

        @pl.when(middle)
        def _():
            @pl.when(n == 1)
            def _():
                near(3, s).start()

            @pl.when(n == 2)
            def _():
                mid_first(3)

                @pl.when(h == s)
                def _():
                    wo_turned()
                    wo_out(s == 1)

            @pl.when(n == 3)
            def _():
                mid_second(3)

        @pl.when(n == 3)
        def _():
            halo_out_pieces(range(HALO_FIRST, NS))

            @pl.when(jnp.logical_and(middle, h == s))
            def _():
                wo_out(s == 2)

        @pl.when(middle)
        def _():
            @pl.when(h == near_dev)
            def _():
                plan(n, MID_W_EARLY, wrelay)

            @pl.when(jnp.logical_and(h != near_dev, h != s))
            def _():
                plan(n, MID_W, wrelay)
        plan(n, HALO_SPREAD, halo_spread)
        plan(n, HALO_PASS, halo_pass)

    def slot(n, _):
        t, g = n // units, lax.rem(n, units)

        @pl.when(g == 0)
        def _():
            if COMM:
                twin_span = G.at[t, pl.ds(0, (S - 1) * RH), :]
                rcopy(twin_span, twin_span, send_x, xr.at[t], dev(s, h, 1 - b)).wait_recv()
            if COMP:
                queries(t)
        if COMP:
            unit(t, g)
        if COMM:
            att_send(t, g)
            events(n)

            @pl.when(t > 0)
            def _():
                att_pass(t - 1, g)
        return 0

    lax.fori_loop(0, NS * units, slot, 0)

    def edge_w(ks):
        @pl.when(jnp.logical_and(edge, h != s))
        def _():
            for k in ks:
                wrelay(k)

    def wrows(n):
        return WO.at[:, pl.ds(0, n * KQ // NS), :]

    def wx_got(i, n):
        @pl.when(h != s)
        def _():
            rcopy(wrows(n), wrows(n), wsend_x, wxr.at[i], dev(s, h, 1 - b)).wait_recv()

    def gathered(ts, rows):
        return jnp.concatenate([att[t, k, rows, :] for t in ts for k in range(H)], axis=1)

    early = range(NS - 1)

    def fold_early(g, _):
        r = pl.ds(blk + g * GR, GR)
        acc[r, :] = jnp.dot(gathered(early, r), WO[0:NS - 1].reshape((NS - 1) * H * CW, -1),
                            preferred_element_type=F32)
        return 0

    if COMM:
        edge_w(EDGE_W_TAIL[0])
        plan(NS * units, HALO_PASS, halo_pass)
        edge_w(EDGE_W_TAIL[1])

        @pl.when(s > 0)
        def _():
            half = halo_in.at[pl.ds(0, HR)]
            rcopy(half, half, hm_s, hm_r, dev(s, mate, b)).wait_recv()
    if COMP:
        attend_all([(t, 0, project(t, halo_in[...])) for t in range(NS)])
    if COMM:
        for k in range(3):
            att_first(k, peers[k]).start()
        edge_w(EDGE_W_TAIL[2])
        for g in range(units):
            att_pass(NS - 1, g)
        for t in early:
            att_got(t)
        wx_got(0, NX - 1)
    if COMP:
        lax.fori_loop(0, units, fold_early, 0)
    if COMM:
        edge_w(EDGE_W_TAIL[3])
        wx_got(1, 1)
        att_got(NS - 1)

    def fold_late(g, _):
        r = pl.ds(blk + g * GR, GR)
        if COMP:
            part = jnp.dot(gathered((NS - 1,), r), WO[NS - 1], preferred_element_type=F32)
            out[r, :] = (acc[r, :] + part).astype(BF16)
        return 0
    lax.fori_loop(0, units, fold_late, 0)
    if COMM:
        for k in range(3):
            att_first(k, peers[k]).wait_recv()
    first = pl.ds(0, blk)
    if COMP:
        out[first, :] = jnp.dot(gathered(range(NS), first), WO[...].reshape(NS * H * CW, -1),
                                preferred_element_type=F32).astype(BF16)

    def drained(span, sem, device):
        rcopy(span, span, sem, hm_r, device).wait_send()

    if COMM:
        beside = dev(s, mate, b)

        @pl.when(edge)
        def _():
            drained(G.at[:, pl.ds(0, RH), :], send_n, beside)

        @pl.when(middle)
        def _():
            drained(G.at[:, pl.ds(0, 3 * RH), :], send_n, beside)
            drained(G.at[:, pl.ds(0, 2 * RH), :], send_f, beside)
        drained(G.at[:, pl.ds(0, (S - 1) * RH), :], send_x, beside)
        drained(att.at[:, 0:3], att_s, beside)

        @pl.when(jnp.logical_and(lead, s < S - 1))
        def _():
            drained(halo_out, hz_s, beside)

        @pl.when(s > 0)
        def _():
            drained(halo_in.at[pl.ds(0, HR)], hm_s, beside)

            @pl.when(lead)
            def _():
                drained(halo_in.at[pl.ds(0, HR)], hy_s, beside)

        @pl.when(jnp.logical_and(s >= h, s < S - 1))
        def _():
            drained(wrows(NZ), wsend_r, beside)

        @pl.when(jnp.logical_and(s <= h, s > 0))
        def _():
            drained(wrows(NZ), wsend_l, beside)

        @pl.when(h != s)
        def _():
            drained(wrows(NX), wsend_x, beside)
            drained(w_out, turn_s, beside)
    else:
        @pl.when(h == s)
        def _():
            wo_own.wait()


def one_kernel(tokens, neighbor_bank, slots, w_query, w_key, w_value, w_out):
    S, H = lax.axis_size("seq"), lax.axis_size("head")
    T, D = tokens.shape
    nblk, nrow = neighbor_bank.shape[:2]
    width = w_query.shape[1]
    NS = width // HEAD_DIM
    CW = HEAD_DIM
    out_cols = D // H
    dma = pltpu.SemaphoreType.DMA
    hbm = pl.BlockSpec(memory_space=pltpu.HBM)
    tokens, neighbor_bank, slots, w_query, w_key, w_value, w_out = [
        pltpu.with_memory_space_constraint(x, pltpu.HBM)
        for x in (tokens, neighbor_bank, slots, w_query, w_key, w_value, w_out.reshape(NS, CW, -1))]
    return pl.pallas_call(
        functools.partial(fused, S, H, NS),
        out_shape=jax.ShapeDtypeStruct((T, out_cols), BF16),
        in_specs=[hbm, hbm, pl.BlockSpec(memory_space=pltpu.SMEM), hbm, hbm, hbm, hbm],
        out_specs=pl.BlockSpec(memory_space=pltpu.VMEM),
        scratch_shapes=[
            pltpu.VMEM((NS, D, 3 * CW), BF16),
            pltpu.VMEM((NS, H * CW, out_cols), BF16),
            pltpu.VMEM((T, D), BF16),
            pltpu.VMEM((T, D), BF16),
            pltpu.VMEM((nblk, nrow, D), BF16),
            pltpu.VMEM((nrow // 2, D), BF16),
            pltpu.VMEM((nrow, D), BF16),
            pltpu.VMEM((NS, T, CW), BF16),
            pltpu.VMEM((NS, H, T, CW), BF16),
            pltpu.VMEM((T, out_cols), F32),
            dma((2,)),
            dma((NS,)),
            dma((NS, S)), dma((NS,)), dma, dma, dma,
            dma((NZ,)), dma((2,)), dma, dma, dma, dma, dma, dma,
            dma, dma((NS,)), dma, dma((NS,)), dma, dma,
            dma, dma((NS, 3)), dma((2, NS)), dma((3,)),
        ],
        compiler_params=pltpu.CompilerParams(
            collective_id=0, has_side_effects=True, vmem_limit_bytes=VMEM_MIB * 1024 * 1024),
    )(tokens, neighbor_bank, slots, w_query, w_key, w_value, w_out)


def passed_along(block, axis, distance):
    devices = range(lax.axis_size(axis))
    route = [(i - distance, i) for i in devices if i - distance in devices]
    return lax.ppermute(block, axis, route)


def attend(query_blocks, key_blocks, value_blocks):
    scores = jnp.einsum(
        "cmhd,cnhd->chmn", query_blocks, key_blocks, preferred_element_type=jnp.float32
    ) / math.sqrt(HEAD_DIM)
    peak_score = jnp.max(scores, axis=-1, keepdims=True)
    exponent = jnp.exp(scores - peak_score)
    weights = (exponent / jnp.sum(exponent, axis=-1, keepdims=True)).astype(jnp.bfloat16)
    blended = jnp.einsum(
        "chmn,cnhd->cmhd", weights, value_blocks, preferred_element_type=jnp.float32
    ).astype(jnp.bfloat16)
    return blended.reshape(blended.shape[0] * blended.shape[1], blended.shape[2] * blended.shape[3])


def fold_rows(source, shard_rows):
    return jnp.dot(source, shard_rows, preferred_element_type=jnp.float32)


def local(tokens, neighbor_bank, slots, w_query, w_key, w_value, w_out):
    tok_rows, model_width = tokens.shape
    block_count = neighbor_bank.shape[0]
    neighbor_rows = neighbor_bank.shape[1]
    block_len = tok_rows // block_count
    local_width = w_query.shape[1]
    local_heads = local_width // HEAD_DIM
    hidden = tokens.astype(jnp.float32)
    normed = (hidden * lax.rsqrt(jnp.mean(hidden * hidden, axis=-1, keepdims=True) + 1e-06)).astype(
        jnp.bfloat16
    )
    retrieved = jnp.take(neighbor_bank, slots, axis=0)
    arrived = passed_along(retrieved[block_count - 1], "seq", 1)
    context = jnp.concatenate([arrived[None], retrieved[: block_count - 1]], axis=0)
    context_flat = context.reshape(block_count * neighbor_rows, model_width)
    query_sum = fold_rows(normed, lax.all_gather(w_query, "seq", axis=0, tiled=True))
    key_sum = fold_rows(context_flat, lax.all_gather(w_key, "seq", axis=0, tiled=True))
    value_sum = fold_rows(context_flat, lax.all_gather(w_value, "seq", axis=0, tiled=True))
    query_blocks = query_sum.astype(jnp.bfloat16).reshape(
        block_count, block_len, local_heads, HEAD_DIM
    )
    key_blocks = key_sum.astype(jnp.bfloat16).reshape(
        block_count, neighbor_rows, local_heads, HEAD_DIM
    )
    value_blocks = value_sum.astype(jnp.bfloat16).reshape(
        block_count, neighbor_rows, local_heads, HEAD_DIM
    )
    attended = attend(query_blocks, key_blocks, value_blocks)
    every_head = lax.all_gather(attended, "head", axis=1, tiled=True)
    wide_rows = lax.all_gather(w_out, "seq", axis=1, tiled=True)
    own_columns = lax.all_to_all(wide_rows, "head", split_axis=1, concat_axis=0, tiled=True)
    return jnp.dot(every_head, own_columns, preferred_element_type=jnp.float32).astype(jnp.bfloat16)


def solution(mesh):
    in_specs = (
        P(("batch", "seq"), None),
        P(("batch", "seq"), None, None),
        P(("batch", "seq")),
        P("seq", "head"),
        P("seq", "head"),
        P("seq", "head"),
        P("head", "seq"),
    )
    out_specs = P(("batch", "seq"), "head")
    square = mesh.shape["seq"] == 4 and mesh.shape["head"] == 4 and mesh.shape["batch"] == 2
    body = one_kernel if square else local
    return jax.shard_map(body, mesh=mesh, in_specs=in_specs, out_specs=out_specs, check_vma=False)
```

time: 107 us -> 86.3 us (0.81)
  Pallas kernels: 105 us -> 85.1 us
  local copies, waits for them, and re-layouts: 2.26 us -> 0.97 us
    pallas_call x1, Pallas kernels: 105 us -> 85.1 us  [one_kernel(): pl.pallas_call(functools.partial(fused, S, H, NS), out_shape=jax.ShapeDty...]
    unnamed x1, local copies, waits for them, and re-layouts: 2.26 us -> 0.97 us
where the time goes in v2:
time: 86.3 us; the launch traced here: 86.1 us
  Pallas kernels  85.1 us (99%)
  local copies, waits for them, and re-layouts  0.97 us (1%)
    pallas_call x1, Pallas kernels, one_kernel(): pl.pallas_call(functools.partial(fused, S, H, NS), out_shape=jax.ShapeDty...  85.1 us

profile of v2, /device:TPU:25, one launch (start us, length us, event | category | flops | bytes accessed | tf_op | source)
XLA Modules:
  0.0 86.1 jit_solution(14944749041251495027)
XLA Ops:
  0.0 85.1 %shard_map.73 = bf16[1024,512]{1,0:T(8,128)(2,1)S(1)} custom-call(bf16[1024,2048]{1,0:T(8,128)(2,1)} %tokens.1, bf16[16,256,2048]{2,1,0:T(8,128)(2,1)} %bank.1, s32[16]{0:T(128)} %slots.1, bf16[512,512]{1,0:T(8,128)(2,1)} %w_query.1, bf16[512,512]{1,0:T(8,128)(2,1)} %w_key.1, bf16[512,512]{1,0:T(8,128)(2,1)} %w_value.1, bf16[4,128,512]{2,1,0:T(8,128)(2,1)} %bitcast.1), custom_call_target="tpu_custom_call" | custom-call | tf_op jit(solution)/shard_map/pallas_call | solution.py:592
  85.1 1.0 %copy.9 = bf16[1024,512]{1,0:T(8,128)(2,1)} copy(bf16[1024,512]{1,0:T(8,128)(2,1)S(1)} %shard_map.73) | data formatting | bytes 2097152

commit v3 on v2

--- a/solution.py
+++ b/solution.py
@@ -14,25 +14,33 @@
 
 
 NZ, NX = 9, 7
-HALO_FIRST = 2
-EDGE_QKV = {0: ((1, 2),), 1: ((1, 3),), 2: ((2, 2),), 3: ((2, 3),), 4: ((3, 1),), 5: ((3, 2),), 6: ((3, 3),)}
-EDGE_W = {7: (0,), 8: (1,), 9: (2,), 10: (3,), 11: (4,)}
-EDGE_W_LATE = {9: (0, 1), 10: (2,), 11: (3, 4)}
-EDGE_W_TAIL = ((5,), (), (6,), (7, 8))
+EDGE_QKV = {0: ((1, 2),), 2: ((1, 3),), 3: ((2, 2),), 5: ((2, 3),), 6: ((3, 1),), 7: ((3, 2),), 9: ((3, 3),)}
+EDGE_W = {10: (1,), 11: (2,), 12: (3,), 14: (4,), 15: (5,)}
+EDGE_W_OUT = {0: (1, 2), 1: (3,), 2: (4,), 3: (5,), 4: (6,), 5: (7, 8)}
+EDGE_W_TAIL = ((), (6,), (7, 8))
+MID_QKV = {0: ((1, 2),), 2: ((2, 2),), 3: ((3, 3),), 4: ((1, 3),), 6: ((2, 3),)}
+MID_W_EARLY = {3: (1,), 4: (2,), 5: (3,), 6: (4,), 7: (5,), 8: (6,), 9: (7, 8)}
+MID_W = {8: (1,), 9: (2,), 10: (3,), 11: (4,), 12: (5,), 13: (6,), 14: (7, 8)}
+EDGE_W_FREE = {11: (0,), 12: (1, 2), 13: (3,), 14: (4,), 15: (5,)}
+MID_W_FREE = {8: (0,), 9: (1,), 10: (2, 3), 11: (4,), 12: (5, 6), 13: (7, 8)}
+V_EDGE_OPEN = {1: (0,)}
+V_MID_OPEN = {3: (0,)}
+V_MID_FAR = {4: (0,)}
+V_MID_NEAR = {8: (0,)}
+V_EDGE = {10: (0,)}
+V_FINISH = {12: (0,)}
 VMEM_MIB = 48
-MID_W_EARLY = {2: (0, 1), 3: (2, 3), 4: (4, 5), 5: (6, 7, 8)}
-MID_W = {5: (0, 1), 6: (2, 3, 4), 7: (5,), 8: (6,), 9: (7, 8)}
-HALO_SPREAD = {5: (0, 1), 8: (2, 3)}
-HALO_PASS = {8: (0,), 9: (1,), 12: (2, 3)}
+NQ = 2
 COMM = True
 COMP = True
 
 
 def fused(S, H, NS, tokens, bank, slots, w_query, w_key, w_value, w_out, out,
-          G, WO, tok, normed, rows_in, halo_out, halo_in, qb, att, acc,
+          G, WO, VB, tok, normed, rows_in, qb, att, acc,
           ld_sem, wl_sem, zr, xr, send_n, send_f, send_x,
           wzr, wxr, wsend_r, wsend_l, wsend_x, turn_s, turn_r, turn_l,
-          hz_s, hz_r, hy_s, hy_r, hm_s, hm_r, att_s, att_y, att_m, att_b):
+          hq_s, hq_r, ha_s, ha_r, att_s, att_y, att_m, att_b,
+          vt_s, vt_r, vt_l, vz_s, vz_r, vx_s, vx_r, vy_s, vy_r):
     s, h, b = lax.axis_index("seq"), lax.axis_index("head"), lax.axis_index("batch")
     nblk, nrow, D = bank.shape
     T = tokens.shape[0]
@@ -43,11 +51,9 @@
     KH = H * CW // 2
     KQ = KH // 2
     NW = 2 * NS
-    units = 3
-    per = (nblk - 1) // units
+    units = NS
+    per = nblk // units
     GR = per * blk
-    HR = nrow // 2
-    HP = HR // NS
 
     def dev(seq, head, batch):
         return {"seq": seq, "head": head, "batch": batch}
@@ -63,7 +69,6 @@
     far_dev = 3 - s
     edge_dev = 1 + s // 3
     side = lax.rem(h, 2)
-    lead = h >= H // 2
     mate = (h // 2) * 2 + 1 - side
     across = lax.rem(h + 2, H)
     peers = (mate, across, lax.rem(mate + 2, H))
@@ -102,50 +107,56 @@
         greet(dev(far_dev, h, b))
         pl.semaphore_wait(barrier, 6)
 
-    def chunk(t, origin, half):
-        return G.at[t, pl.ds(origin * RS + half * RH, RH), :]
-
-    def near(t, origin):
-        return rcopy(chunk(t, origin, b), chunk(t, origin, b), send_n, zr.at[t, origin],
+    RQ = RH // NQ
+
+    def chunk(t, origin, half, q):
+        return G.at[t, pl.ds(origin * RS + half * RH + q * RQ, RQ), :]
+
+    def near(t, origin, q):
+        return rcopy(chunk(t, origin, b, q), chunk(t, origin, b, q), send_n, zr.at[t, origin, q],
                      dev(near_dev, h, b))
 
-    def far(t, origin):
-        return rcopy(chunk(t, origin, b), chunk(t, origin, b), send_f, zr.at[t, origin],
+    def far(t, origin, q):
+        return rcopy(chunk(t, origin, b, q), chunk(t, origin, b, q), send_f, zr.at[t, origin, q],
                      dev(far_dev, h, b))
 
-    def inward(t, origin):
-        return rcopy(chunk(t, origin, b), chunk(t, origin, b), send_n, zr.at[t, origin],
+    def inward(t, origin, q):
+        return rcopy(chunk(t, origin, b, q), chunk(t, origin, b, q), send_n, zr.at[t, origin, q],
                      dev(edge_dev, h, b))
 
-    def twin(t, origin, half):
-        return rcopy(chunk(t, origin, half), chunk(t, origin, half), send_x, xr.at[t],
-                     dev(s, h, 1 - b))
+    def twin(t, origin, q):
+        return rcopy(chunk(t, origin, b, q), chunk(t, origin, b, q), send_x, xr.at[t], dev(s, h, 1 - b))
+
+    def send_own(way, t):
+        for q in range(NQ):
+            way(t, s, q).start()
 
     def edge_event(t, d):
         o = d + (s // 3) * (3 - 2 * d)
-        inward(t, o).wait_recv()
-        twin(t, o, b).start()
+        for q in range(NQ):
+            inward(t, o, q).wait_recv()
+            twin(t, o, q).start()
+
+    def forward(way, t, o, q):
+        way(t, o, q).wait_recv()
+        way(t, o, q).start()
+        twin(t, o, q).start()
 
     def mid_first(t):
         a, e = 3 - s, 3 * (s - 1)
-
-        def outer():
-            far(t, e).wait_recv()
-            far(t, e).start()
-            twin(t, e, b).start()
-        if t > 0:
-            outer()
-        far(t, a).wait_recv()
-        near(t, a).start()
-        twin(t, a, b).start()
         if t == 0:
-            outer()
+            for q in range(NQ):
+                forward(near, t, a, q)
+                forward(far, t, e, q)
+        else:
+            for q in range(NQ):
+                forward(far, t, e, q)
+            for q in range(NQ):
+                forward(near, t, a, q)
 
     def mid_second(t):
-        o = 3 * (2 - s)
-        near(t, o).wait_recv()
-        near(t, o).start()
-        twin(t, o, b).start()
+        for q in range(NQ):
+            forward(near, t, 3 * (2 - s), q)
 
     def turn(j, device):
         return rcopy(w_out, WO.at[:, pl.ds(j * CW, CW), :], turn_s, turn_r, device)
@@ -164,21 +175,76 @@
 
     def wtwin(k, half):
         return rcopy(wpart(k, half), wpart(k, half), wsend_x, wxr.at[k // (NX - 1)], dev(s, h, 1 - b))
+
+    def crowded(who):
+        return jnp.logical_or(jnp.logical_and(who < H // 2, s > who), jnp.logical_and(who >= H // 2, s < who))
+
+    crowd = crowded(h)
+    carries = crowded(across)
+    opens = s == across
+    carrier = lax.rem(s + 2, H)
+
+    def vturn(j, device):
+        return rcopy(w_out.at[0], VB.at[j // 2], vt_s, vt_r, device)
+
+    def vturn_here():
+        return pltpu.make_async_copy(w_out.at[0], VB.at[h // 2], vt_l)
+
+    def vz(k):
+        return rcopy(VB.at[b], VB.at[b], vz_s, vz_r,
+                     dev(lax.rem(s + S + 1 - 2 * (across // 2), S), h, b))
+
+    def vx(k):
+        return rcopy(VB.at[b], VB.at[b], vx_s, vx_r, dev(s, h, 1 - b))
+
+    def vy(k, half):
+        return rcopy(VB.at[half], WO.at[0, pl.ds(half * KH, KQ), :], vy_s, vy_r, dev(s, across, b))
+
+    def v_open():
+        @pl.when(opens)
+        def _():
+            @pl.when(side == 0)
+            def _():
+                vturn_here().wait()
+                rcopy(VB.at[0], VB.at[0], vt_s, vt_r, dev(s, mate, b)).wait_recv()
+
+            @pl.when(side == 1)
+            def _():
+                rcopy(VB, VB, vt_s, vt_r, dev(s, mate, b)).wait_recv()
+            vz(0).start()
+
+    onward = jnp.logical_or(jnp.logical_and(across < H // 2, s < S - 1), jnp.logical_and(across >= H // 2, s > 0))
+
+    def v_relay(k):
+        @pl.when(carries)
+        def _():
+            vz(k).wait_recv()
+
+            @pl.when(onward)
+            def _():
+                vz(k).start()
+            vx(k).start()
+            vy(k, b).start()
+
+    def v_finish():
+        @pl.when(carries)
+        def _():
+            rcopy(VB.at[0], VB.at[0], vx_s, vx_r, dev(s, h, 1 - b)).wait_recv()
+            vy(0, 1 - b).start()
 
     def wo_turned():
         wo_own.wait()
         three = WO.at[:, pl.ds(0, (H - 1) * CW), :]
         rcopy(three, three, turn_s, turn_r, dev(s, mate, b)).wait_recv()
 
-    def wo_out(rightward):
-        for k in range(NZ):
-            @pl.when(jnp.logical_and(rightward, s < S - 1))
-            def _():
-                wright(k).start()
-
-            @pl.when(jnp.logical_and(jnp.logical_not(rightward), s > 0))
-            def _():
-                wleft(k).start()
+    def wo_out(rightward, k):
+        @pl.when(jnp.logical_and(rightward, s < S - 1))
+        def _():
+            wright(k).start()
+
+        @pl.when(jnp.logical_and(jnp.logical_not(rightward), s > 0))
+        def _():
+            wleft(k).start()
 
     def wrelay(k):
         wright(k).wait_recv()
@@ -193,35 +259,15 @@
         if k < NX:
             wtwin(k, b).start()
 
-    def halo_part(p, who):
-        return halo_in.at[pl.ds(who * HR + p * HP, HP)]
-
-    def halo_z(p):
-        return rcopy(halo_out.at[pl.ds(p * HP, HP)], halo_part(p, side), hz_s, hz_r.at[p],
+    def ask(t):
+        return rcopy(qb.at[t, pl.ds(0, blk), :], qb.at[t, pl.ds(T, blk), :], hq_s, hq_r.at[t],
+                     dev(lax.rem(s + S - 1, S), h, b))
+
+    def answer(t):
+        return rcopy(att.at[t, h, pl.ds(T, blk), :], att.at[t, h, pl.ds(0, blk), :], ha_s, ha_r.at[t],
                      dev(lax.rem(s + 1, S), h, b))
 
-    def halo_y(p):
-        return rcopy(halo_part(p, side), halo_part(p, side), hy_s, hy_r.at[p], dev(s, across, b))
-
-    def halo_m(p, who):
-        return rcopy(halo_part(p, who), halo_part(p, who), hm_s, hm_r, dev(s, mate, b))
-
-    def halo_spread(p):
-        @pl.when(jnp.logical_and(lead, s > 0))
-        def _():
-            halo_z(p).wait_recv()
-            halo_y(p).start()
-            halo_m(p, side).start()
-
-    def halo_pass(p):
-        @pl.when(jnp.logical_and(jnp.logical_not(lead), s > 0))
-        def _():
-            halo_y(p).wait_recv()
-            halo_m(p, side).start()
-
     def att_rows(t, who, g):
-        if isinstance(g, int) and g == units:
-            return att.at[t, who, pl.ds(0, blk), :]
         return att.at[t, who, pl.ds(blk + g * GR, GR), :]
 
     def att_copy(t, g, who, rs, device):
@@ -237,12 +283,26 @@
 
     def att_got(t):
         for k in range(2):
-            block = att.at[t, 0, pl.ds(blk, T - blk), :]
+            block = att.at[t, 0, pl.ds(blk, T), :]
             rcopy(block, block, att_s, att_m.at[k, t], dev(s, mate, b)).wait_recv()
 
-    def att_first(k, device):
-        part = att.at[:, h, pl.ds(0, blk), :]
-        return rcopy(part, part, att_s, att_b.at[k], dev(s, device, b))
+    def att_first(t, k, who, device):
+        part = att.at[t, who, pl.ds(0, blk), :]
+        return rcopy(part, part, att_s, att_b.at[k, t // (NS - 1)], dev(s, device, b))
+
+    def first_out(t):
+        @pl.when(s > 0)
+        def _():
+            answer(t).wait_recv()
+            for k in range(3):
+                att_first(t, k, h, peers[k]).start()
+
+    def first_got(i, n):
+        @pl.when(s > 0)
+        def _():
+            for k in range(3):
+                part = att.at[0:n, 0, pl.ds(0, blk), :]
+                rcopy(part, part, att_s, att_b.at[k, i], dev(s, peers[k], b)).wait_recv()
 
     scale = math.log2(math.e) / math.sqrt(HEAD_DIM)
 
@@ -267,7 +327,7 @@
         attend_all([(t, first + i, kv[i * nrow:(i + 1) * nrow]) for i in range(per)])
 
     def queries(t):
-        qb[t] = jnp.dot(normed[...], G[t, :, pl.ds(0, CW)], preferred_element_type=F32).astype(BF16)
+        qb[t, pl.ds(0, T), :] = jnp.dot(normed[...], G[t, :, pl.ds(0, CW)], preferred_element_type=F32).astype(BF16)
 
     def loaded(j):
         own = G.at[j, pl.ds(s * RS, RS), :]
@@ -279,12 +339,12 @@
     if COMM:
         @pl.when(middle)
         def _():
-            near(0, s).start()
-            far(0, s).start()
+            send_own(near, 0)
+            send_own(far, 0)
 
         @pl.when(edge)
         def _():
-            inward(0, s).start()
+            send_own(inward, 0)
     loaded(1)
     tok_load.start()
 
@@ -296,29 +356,37 @@
     if COMM:
         @pl.when(middle)
         def _():
-            near(1, s).start()
+            send_own(near, 1)
 
         @pl.when(edge)
         def _():
-            inward(1, s).start()
+            send_own(inward, 1)
 
         @pl.when(h != s)
         def _():
             turn(h, dev(s, s, b)).start()
+
+        @pl.when(jnp.logical_and(opens, side == 0))
+        def _():
+            vturn_here().start()
+
+        @pl.when(jnp.logical_and(jnp.logical_not(opens), side == 0))
+        def _():
+            vturn(h, dev(s, carrier, b)).start()
     loaded(2)
     loaded(3)
     if COMM:
         @pl.when(edge)
         def _():
-            inward(2, s).start()
-            inward(3, s).start()
+            send_own(inward, 2)
+            send_own(inward, 3)
 
             edge_event(0, 1)
 
         @pl.when(middle)
         def _():
             mid_first(0)
-            far(1, s).start()
+            send_own(far, 1)
     tok_load.wait()
 
     def norm(i, _):
@@ -331,13 +399,13 @@
 
     pltpu.make_async_copy(bank, rows_in, ld_sem.at[0]).wait()
     if COMM:
-        @pl.when(jnp.logical_and(lead, s < S - 1))
-        def _():
-            halo_out[...] = rows_in[slots[nblk - 1], pl.ds(side * HR, HR), :]
+        @pl.when(s == S - 1)
+        def _():
+            qb[:, pl.ds(T, blk), :] = jnp.zeros((NS, blk, CW), BF16)
 
         @pl.when(s == 0)
         def _():
-            halo_in[...] = jnp.zeros_like(halo_in)
+            att[:, :, pl.ds(0, blk), :] = jnp.zeros((NS, H, blk, CW), BF16)
 
         @pl.when(edge)
         def _():
@@ -347,88 +415,62 @@
             @pl.when(h == s)
             def _():
                 wo_turned()
-                wo_out(s == 0)
 
         @pl.when(middle)
         def _():
             mid_second(0)
-            near(2, s).start()
+            send_own(near, 2)
             mid_first(1)
-            far(2, s).start()
+            send_own(far, 2)
             mid_second(1)
 
-    def halo_out_pieces(pieces):
-        @pl.when(jnp.logical_and(lead, s < S - 1))
-        def _():
-            for p in pieces:
-                halo_z(p).start()
-
     def plan(n, table, event):
+        t, g = n
         for at, items in table.items():
-            @pl.when(n == at)
-            def _():
-                for item in items:
-                    event(item)
+            if at % units == g:
+                @pl.when(t == at // units)
+                def _():
+                    for item in items:
+                        event(item)
 
     def events(n):
         @pl.when(edge)
         def _():
             plan(n, EDGE_QKV, lambda e: edge_event(*e))
-
-            late = jnp.logical_and(s == S - 1, lead)
-
-            @pl.when(jnp.logical_and(h != s, jnp.logical_not(late)))
+            plan(n, V_EDGE_OPEN, lambda e: v_open())
+
+            @pl.when(crowd)
             def _():
                 plan(n, EDGE_W, wrelay)
 
-            @pl.when(jnp.logical_and(h != s, late))
-            def _():
-                plan(n, EDGE_W_LATE, wrelay)
+            @pl.when(h == s)
+            def _():
+                plan(n, EDGE_W_OUT, lambda k: wo_out(s == 0, k))
+
+            @pl.when(jnp.logical_not(jnp.logical_or(crowd, h == s)))
+            def _():
+                plan(n, EDGE_W_FREE, wrelay)
+            plan(n, V_EDGE, v_relay)
 
         @pl.when(middle)
         def _():
-            @pl.when(n == 0)
-            def _():
-                mid_first(2)
-                far(3, s).start()
-
-            @pl.when(n == 1)
-            def _():
-                mid_second(2)
-
-        @pl.when(n == 1)
-        def _():
-            halo_out_pieces(range(HALO_FIRST))
-
-        @pl.when(middle)
-        def _():
-            @pl.when(n == 1)
-            def _():
-                near(3, s).start()
-
-            @pl.when(n == 2)
-            def _():
-                mid_first(3)
-
-                @pl.when(h == s)
-                def _():
-                    wo_turned()
-                    wo_out(s == 1)
-
-            @pl.when(n == 3)
-            def _():
-                mid_second(3)
-
-        @pl.when(n == 3)
-        def _():
-            halo_out_pieces(range(HALO_FIRST, NS))
-
-            @pl.when(jnp.logical_and(middle, h == s))
-            def _():
-                wo_out(s == 2)
-
-        @pl.when(middle)
-        def _():
+            plan(n, MID_QKV, lambda e: mid_step(*e))
+
+            @pl.when(h == s)
+            def _():
+                plan(n, {2: (0,)}, lambda k: wo_turned())
+                plan(n, MID_W_EARLY, lambda k: wo_out(s == 1, k))
+                plan(n, MID_W_FREE, lambda k: wo_out(s == 2, k))
+            plan(n, V_MID_OPEN, lambda e: v_open())
+
+            @pl.when(across == near_dev)
+            def _():
+                plan(n, V_MID_FAR, v_relay)
+
+            @pl.when(across != near_dev)
+            def _():
+                plan(n, V_MID_NEAR, v_relay)
+
             @pl.when(h == near_dev)
             def _():
                 plan(n, MID_W_EARLY, wrelay)
@@ -436,11 +478,22 @@
             @pl.when(jnp.logical_and(h != near_dev, h != s))
             def _():
                 plan(n, MID_W, wrelay)
-        plan(n, HALO_SPREAD, halo_spread)
-        plan(n, HALO_PASS, halo_pass)
+        plan(n, V_FINISH, lambda e: v_finish())
+
+    def mid_step(kind, t):
+        if kind == 1:
+            mid_first(t)
+            if t < NS - 1:
+                send_own(far, t + 1)
+        elif kind == 2:
+            mid_second(t)
+        else:
+            send_own(near, t)
 
     def slot(n, _):
         t, g = n // units, lax.rem(n, units)
+        u = g + (s // 2) * (((g + 1) // 2) * (1 - g // 2) * 2 - g // 2)
+        asked = jnp.logical_and(u == units - 1, s < S - 1)
 
         @pl.when(g == 0)
         def _():
@@ -449,15 +502,34 @@
                 rcopy(twin_span, twin_span, send_x, xr.at[t], dev(s, h, 1 - b)).wait_recv()
             if COMP:
                 queries(t)
+            if COMM:
+                @pl.when(s > 0)
+                def _():
+                    ask(t).start()
+        if COMM:
+            @pl.when(asked)
+            def _():
+                ask(t).wait_recv()
         if COMP:
-            unit(t, g)
+            unit(t, u)
         if COMM:
-            att_send(t, g)
-            events(n)
+            att_send(t, u)
+
+            @pl.when(asked)
+            def _():
+                answer(t).start()
+            for i in range(units):
+                @pl.when(g == i)
+                def _():
+                    events((t, i))
 
             @pl.when(t > 0)
             def _():
-                att_pass(t - 1, g)
+                att_pass(t - 1, u)
+
+                @pl.when(g == units - 1)
+                def _():
+                    first_out(t - 1)
         return 0
 
     lax.fori_loop(0, NS * units, slot, 0)
@@ -471,10 +543,23 @@
     def wrows(n):
         return WO.at[:, pl.ds(0, n * KQ // NS), :]
 
+    def wx_wait(i, n):
+        rcopy(wrows(n), wrows(n), wsend_x, wxr.at[i], dev(s, h, 1 - b)).wait_recv()
+
     def wx_got(i, n):
-        @pl.when(h != s)
-        def _():
-            rcopy(wrows(n), wrows(n), wsend_x, wxr.at[i], dev(s, h, 1 - b)).wait_recv()
+        if i == 0:
+            @pl.when(crowd)
+            def _():
+                wx_wait(i, n - 1)
+                rcopy(VB, VB, vy_s, vy_r, dev(s, across, b)).wait_recv()
+
+            @pl.when(jnp.logical_not(jnp.logical_or(crowd, h == s)))
+            def _():
+                wx_wait(i, n)
+        else:
+            @pl.when(h != s)
+            def _():
+                wx_wait(i, n)
 
     def gathered(ts, rows):
         return jnp.concatenate([att[t, k, rows, :] for t in ts for k in range(H)], axis=1)
@@ -482,55 +567,39 @@
     early = range(NS - 1)
 
     def fold_early(g, _):
-        r = pl.ds(blk + g * GR, GR)
+        r = pl.ds(g * GR, GR)
         acc[r, :] = jnp.dot(gathered(early, r), WO[0:NS - 1].reshape((NS - 1) * H * CW, -1),
                             preferred_element_type=F32)
         return 0
 
     if COMM:
         edge_w(EDGE_W_TAIL[0])
-        plan(NS * units, HALO_PASS, halo_pass)
-        edge_w(EDGE_W_TAIL[1])
-
-        @pl.when(s > 0)
-        def _():
-            half = halo_in.at[pl.ds(0, HR)]
-            rcopy(half, half, hm_s, hm_r, dev(s, mate, b)).wait_recv()
-    if COMP:
-        attend_all([(t, 0, project(t, halo_in[...])) for t in range(NS)])
-    if COMM:
-        for k in range(3):
-            att_first(k, peers[k]).start()
-        edge_w(EDGE_W_TAIL[2])
         for g in range(units):
             att_pass(NS - 1, g)
+        first_out(NS - 1)
         for t in early:
             att_got(t)
+        first_got(0, NS - 1)
+        edge_w(EDGE_W_TAIL[1])
         wx_got(0, NX - 1)
     if COMP:
         lax.fori_loop(0, units, fold_early, 0)
     if COMM:
-        edge_w(EDGE_W_TAIL[3])
+        att_got(NS - 1)
+        first_got(1, 1)
+        edge_w(EDGE_W_TAIL[2])
         wx_got(1, 1)
-        att_got(NS - 1)
 
     def fold_late(g, _):
-        r = pl.ds(blk + g * GR, GR)
+        r = pl.ds(g * GR, GR)
         if COMP:
             part = jnp.dot(gathered((NS - 1,), r), WO[NS - 1], preferred_element_type=F32)
             out[r, :] = (acc[r, :] + part).astype(BF16)
         return 0
     lax.fori_loop(0, units, fold_late, 0)
-    if COMM:
-        for k in range(3):
-            att_first(k, peers[k]).wait_recv()
-    first = pl.ds(0, blk)
-    if COMP:
-        out[first, :] = jnp.dot(gathered(range(NS), first), WO[...].reshape(NS * H * CW, -1),
-                                preferred_element_type=F32).astype(BF16)
 
     def drained(span, sem, device):
-        rcopy(span, span, sem, hm_r, device).wait_send()
+        rcopy(span, span, sem, turn_r, device).wait_send()
 
     if COMM:
         beside = dev(s, mate, b)
@@ -544,32 +613,64 @@
             drained(G.at[:, pl.ds(0, 3 * RH), :], send_n, beside)
             drained(G.at[:, pl.ds(0, 2 * RH), :], send_f, beside)
         drained(G.at[:, pl.ds(0, (S - 1) * RH), :], send_x, beside)
-        drained(att.at[:, 0:3], att_s, beside)
-
-        @pl.when(jnp.logical_and(lead, s < S - 1))
-        def _():
-            drained(halo_out, hz_s, beside)
+        drained(att.at[:, 0:3, pl.ds(0, T)], att_s, beside)
+        firsts = att.at[:, 0, pl.ds(0, blk), :]
 
         @pl.when(s > 0)
         def _():
-            drained(halo_in.at[pl.ds(0, HR)], hm_s, beside)
-
-            @pl.when(lead)
-            def _():
-                drained(halo_in.at[pl.ds(0, HR)], hy_s, beside)
+            drained(att.at[:, 0:3, pl.ds(0, blk)], att_s, beside)
+            drained(firsts, hq_s, beside)
+
+        @pl.when(s < S - 1)
+        def _():
+            drained(firsts, ha_s, beside)
+
+        down = h >= H // 2
 
         @pl.when(jnp.logical_and(s >= h, s < S - 1))
         def _():
-            drained(wrows(NZ), wsend_r, beside)
+            @pl.when(down)
+            def _():
+                drained(wrows(NZ), wsend_r, beside)
+
+            @pl.when(jnp.logical_not(down))
+            def _():
+                drained(wrows(NZ - 1), wsend_r, beside)
 
         @pl.when(jnp.logical_and(s <= h, s > 0))
         def _():
-            drained(wrows(NZ), wsend_l, beside)
+            @pl.when(down)
+            def _():
+                drained(wrows(NZ - 1), wsend_l, beside)
+
+            @pl.when(jnp.logical_not(down))
+            def _():
+                drained(wrows(NZ), wsend_l, beside)
+
+        @pl.when(crowd)
+        def _():
+            drained(wrows(NX - 1), wsend_x, beside)
+
+        @pl.when(jnp.logical_not(jnp.logical_or(crowd, h == s)))
+        def _():
+            drained(wrows(NX), wsend_x, beside)
 
         @pl.when(h != s)
         def _():
-            drained(wrows(NX), wsend_x, beside)
             drained(w_out, turn_s, beside)
+
+        @pl.when(jnp.logical_and(jnp.logical_not(opens), side == 0))
+        def _():
+            drained(VB.at[0], vt_s, beside)
+
+        @pl.when(jnp.logical_or(opens, jnp.logical_and(carries, onward)))
+        def _():
+            drained(VB.at[0], vz_s, beside)
+
+        @pl.when(carries)
+        def _():
+            drained(VB.at[0], vx_s, beside)
+            drained(VB, vy_s, beside)
     else:
         @pl.when(h == s)
         def _():
@@ -582,6 +683,7 @@
     nblk, nrow = neighbor_bank.shape[:2]
     width = w_query.shape[1]
     NS = width // HEAD_DIM
+    blk = T // nblk
     CW = HEAD_DIM
     out_cols = D // H
     dma = pltpu.SemaphoreType.DMA
@@ -597,20 +699,20 @@
         scratch_shapes=[
             pltpu.VMEM((NS, D, 3 * CW), BF16),
             pltpu.VMEM((NS, H * CW, out_cols), BF16),
+            pltpu.VMEM((2, CW, out_cols), BF16),
             pltpu.VMEM((T, D), BF16),
             pltpu.VMEM((T, D), BF16),
             pltpu.VMEM((nblk, nrow, D), BF16),
-            pltpu.VMEM((nrow // 2, D), BF16),
-            pltpu.VMEM((nrow, D), BF16),
-            pltpu.VMEM((NS, T, CW), BF16),
-            pltpu.VMEM((NS, H, T, CW), BF16),
+            pltpu.VMEM((NS, T + blk, CW), BF16),
+            pltpu.VMEM((NS, H, T + blk, CW), BF16),
             pltpu.VMEM((T, out_cols), F32),
             dma((2,)),
             dma((NS,)),
-            dma((NS, S)), dma((NS,)), dma, dma, dma,
+            dma((NS, S, NQ)), dma((NS,)), dma, dma, dma,
             dma((NZ,)), dma((2,)), dma, dma, dma, dma, dma, dma,
-            dma, dma((NS,)), dma, dma((NS,)), dma, dma,
-            dma, dma((NS, 3)), dma((2, NS)), dma((3,)),
+            dma, dma((NS,)), dma, dma((NS,)),
+            dma, dma((NS, NS)), dma((2, NS)), dma((3, 2)),
+            dma, dma, dma, dma, dma, dma, dma, dma, dma,
         ],
         compiler_params=pltpu.CompilerParams(
             collective_id=0, has_side_effects=True, vmem_limit_bytes=VMEM_MIB * 1024 * 1024),

time: 86.3 us -> 84.5 us (0.979); the launches traced: 86.1 us -> 82.9 us
  Pallas kernels: 85.1 us -> 81.9 us
    pallas_call x1, Pallas kernels: 85.1 us -> 81.9 us  [one_kernel(): pl.pallas_call(functools.partial(fused, S, H, NS), out_shape=jax.ShapeDty...]
where the time goes in v3:
time: 84.5 us; the launch traced here: 82.9 us
  Pallas kernels  81.9 us (97%)
  local copies, waits for them, and re-layouts  0.97 us (1%)
    pallas_call x1, Pallas kernels, one_kernel(): pl.pallas_call(functools.partial(fused, S, H, NS), out_shape=jax.ShapeDty...  81.9 us

profile of v3, /device:TPU:25, one launch (start us, length us, event | category | flops | bytes accessed | tf_op | source)
XLA Modules:
  0.0 82.9 jit_solution(12443217609827285443)
XLA Ops:
  0.0 81.9 %shard_map.73 = bf16[1024,512]{1,0:T(8,128)(2,1)S(1)} custom-call(bf16[1024,2048]{1,0:T(8,128)(2,1)} %tokens.1, bf16[16,256,2048]{2,1,0:T(8,128)(2,1)} %bank.1, s32[16]{0:T(128)} %slots.1, bf16[512,512]{1,0:T(8,128)(2,1)} %w_query.1, bf16[512,512]{1,0:T(8,128)(2,1)} %w_key.1, bf16[512,512]{1,0:T(8,128)(2,1)} %w_value.1, bf16[4,128,512]{2,1,0:T(8,128)(2,1)} %bitcast.1), custom_call_target="tpu_custom_call" | custom-call | tf_op jit(solution)/shard_map/pallas_call | solution.py:694
  82.0 1.0 %copy.9 = bf16[1024,512]{1,0:T(8,128)(2,1)} copy(bf16[1024,512]{1,0:T(8,128)(2,1)S(1)} %shard_map.73) | data formatting | bytes 2097152

commit v4 on v3

--- a/solution.py
+++ b/solution.py
@@ -26,7 +26,7 @@
 V_EDGE_OPEN = {1: (0,)}
 V_MID_OPEN = {3: (0,)}
 V_MID_FAR = {4: (0,)}
-V_MID_NEAR = {8: (0,)}
+V_MID_NEAR = {7: (0,)}
 V_EDGE = {10: (0,)}
 V_FINISH = {12: (0,)}
 VMEM_MIB = 48
@@ -174,7 +174,7 @@
         return rcopy(wpiece(k), wpiece(k), wsend_l, wzr.at[k], dev(lax.rem(s + S - 1, S), h, b))
 
     def wtwin(k, half):
-        return rcopy(wpart(k, half), wpart(k, half), wsend_x, wxr.at[k // (NX - 1)], dev(s, h, 1 - b))
+        return rcopy(wpart(k, half), wpart(k, half), wsend_x, wxr.at[k // 2], dev(s, h, 1 - b))
 
     def crowded(who):
         return jnp.logical_or(jnp.logical_and(who < H // 2, s > who), jnp.logical_and(who >= H // 2, s < who))
@@ -288,7 +288,7 @@
 
     def att_first(t, k, who, device):
         part = att.at[t, who, pl.ds(0, blk), :]
-        return rcopy(part, part, att_s, att_b.at[k, t // (NS - 1)], dev(s, device, b))
+        return rcopy(part, part, att_s, att_b.at[k, t], dev(s, device, b))
 
     def first_out(t):
         @pl.when(s > 0)
@@ -564,31 +564,42 @@
     def gathered(ts, rows):
         return jnp.concatenate([att[t, k, rows, :] for t in ts for k in range(H)], axis=1)
 
-    early = range(NS - 1)
+    early = (0, 1)
 
     def fold_early(g, _):
         r = pl.ds(g * GR, GR)
-        acc[r, :] = jnp.dot(gathered(early, r), WO[0:NS - 1].reshape((NS - 1) * H * CW, -1),
-                            preferred_element_type=F32)
+        acc[r, :] = jnp.dot(gathered(early, r), WO[0:2].reshape(2 * H * CW, -1), preferred_element_type=F32)
         return 0
 
     if COMM:
-        edge_w(EDGE_W_TAIL[0])
-        for g in range(units):
+        for g in range(2):
             att_pass(NS - 1, g)
-        first_out(NS - 1)
         for t in early:
             att_got(t)
-        first_got(0, NS - 1)
-        edge_w(EDGE_W_TAIL[1])
-        wx_got(0, NX - 1)
+            first_got(t, 1)
+            wx_got(t, 2)
     if COMP:
         lax.fori_loop(0, units, fold_early, 0)
     if COMM:
+        edge_w(EDGE_W_TAIL[1])
+        for g in range(2, units):
+            att_pass(NS - 1, g)
+        first_out(NS - 1)
+        att_got(2)
+        first_got(2, 1)
+        wx_got(2, 2)
+
+    def fold_next(g, _):
+        r = pl.ds(g * GR, GR)
+        acc[r, :] += jnp.dot(gathered((2,), r), WO[2], preferred_element_type=F32)
+        return 0
+    if COMP:
+        lax.fori_loop(0, units, fold_next, 0)
+    if COMM:
+        edge_w(EDGE_W_TAIL[2])
         att_got(NS - 1)
-        first_got(1, 1)
-        edge_w(EDGE_W_TAIL[2])
-        wx_got(1, 1)
+        first_got(NS - 1, 1)
+        wx_got(NS - 1, 1)
 
     def fold_late(g, _):
         r = pl.ds(g * GR, GR)
@@ -709,9 +720,9 @@
             dma((2,)),
             dma((NS,)),
             dma((NS, S, NQ)), dma((NS,)), dma, dma, dma,
-            dma((NZ,)), dma((2,)), dma, dma, dma, dma, dma, dma,
+            dma((NZ,)), dma((NS,)), dma, dma, dma, dma, dma, dma,
             dma, dma((NS,)), dma, dma((NS,)),
-            dma, dma((NS, NS)), dma((2, NS)), dma((3, 2)),
+            dma, dma((NS, NS)), dma((2, NS)), dma((3, NS)),
             dma, dma, dma, dma, dma, dma, dma, dma, dma,
         ],
         compiler_params=pltpu.CompilerParams(

time: 84.5 us -> 83.6 us (0.989)
  no operation moved by 1% of the time
where the time goes in v4:
time: 83.6 us; the launch traced here: 82.3 us
  Pallas kernels  81.4 us (97%)
  local copies, waits for them, and re-layouts  0.97 us (1%)
    pallas_call x1, Pallas kernels, one_kernel(): pl.pallas_call(functools.partial(fused, S, H, NS), out_shape=jax.ShapeDty...  81.4 us

profile of v4, /device:TPU:25, one launch (start us, length us, event | category | flops | bytes accessed | tf_op | source)
XLA Modules:
  0.0 82.3 jit_solution(14024993033176550982)
XLA Ops:
  0.0 81.4 %shard_map.73 = bf16[1024,512]{1,0:T(8,128)(2,1)S(1)} custom-call(bf16[1024,2048]{1,0:T(8,128)(2,1)} %tokens.1, bf16[16,256,2048]{2,1,0:T(8,128)(2,1)} %bank.1, s32[16]{0:T(128)} %slots.1, bf16[512,512]{1,0:T(8,128)(2,1)} %w_query.1, bf16[512,512]{1,0:T(8,128)(2,1)} %w_key.1, bf16[512,512]{1,0:T(8,128)(2,1)} %w_value.1, bf16[4,128,512]{2,1,0:T(8,128)(2,1)} %bitcast.1), custom_call_target="tpu_custom_call" | custom-call | tf_op jit(solution)/shard_map/pallas_call | solution.py:705
  81.4 1.0 %copy.9 = bf16[1024,512]{1,0:T(8,128)(2,1)} copy(bf16[1024,512]{1,0:T(8,128)(2,1)S(1)} %shard_map.73) | data formatting | bytes 2097152
